TPU v7x, 16 devices: a whole 2x2x2 slice. The times are simulated.
16 devices in a mesh: dp: 4 (over z, y), tp: 4 (over x, core).
Axes of the slice: x: 2, y: 2, z: 2, core: 2. Of those that a mesh axis runs over, the one named last changes fastest.
Arguments:
- tokens: int32 [384, 3], P('dp'), parts along dimension 0
- targets: int32 [384, 3], P('dp'), parts along dimension 0
- start_pos: int32 [384], P('dp'), parts along dimension 0
- embed_table: bfloat16 [262144, 1152], P('tp')
- layer_norms: float32 [2, 4, 1152], replicated
- w_q: bfloat16 [2, 1152, 4, 256], replicated
- w_k: bfloat16 [2, 1152, 1, 256], replicated
- w_v: bfloat16 [2, 1152, 1, 256], replicated
- qk_norms: float32 [2, 2, 256], replicated
- w_o: bfloat16 [2, 4, 256, 1152], replicated
- w_gate: bfloat16 [2, 1152, 6912], P(None, None, 'tp')
- w_up: bfloat16 [2, 1152, 6912], P(None, None, 'tp')
- w_down: bfloat16 [2, 6912, 1152], P(None, 'tp')
- norm_final: float32 [1152], replicated
- k_cache: bfloat16 [2, 384, 512, 1, 256], P(None, 'dp'), parts along dimension 1
- v_cache: bfloat16 [2, 384, 512, 1, 256], P(None, 'dp'), parts along dimension 1
Outputs:
- output 1: float32 [384, 3], P('dp'), parts along dimension 0
- output 2: float32 [384, 3], P('dp'), parts along dimension 0
- output 3: bfloat16 [2, 384, 512, 1, 256], P(None, 'dp'), parts along dimension 1
- output 4: bfloat16 [2, 384, 512, 1, 256], P(None, 'dp'), parts along dimension 1
There are 4 independent parts. A program takes and returns all parts, laid end to end along the dimension named above; an argument that names none is the same for every part.
All inputs are finite; a program needn't handle non-finite values.
Results may differ from a plain program's by a relative error of at most 0.0019836.
Values sent between devices are 32-bit elements.
A program may use at most 1.5 GiB of HBM per device.

v0:
```python
import jax
import jax.numpy as jnp
from jax import lax
from jax.sharding import PartitionSpec as P

EPSILON = 1e-6
ROPE_BASE = 10000.0


def rms_norm(values, weight):
    values = values.astype(jnp.float32)
    mean_sq = jnp.mean(values * values, axis=-1, keepdims=True)
    return values * lax.rsqrt(mean_sq + EPSILON) * (1.0 + weight)


def rope_tables(positions, head_dim):
    half_dim = head_dim // 2
    inv_freq = ROPE_BASE ** (-2.0 * jnp.arange(half_dim, dtype=jnp.float32) / head_dim)
    angles = positions.astype(jnp.float32)[:, None] * inv_freq[None, :]
    return jnp.cos(angles)[:, None, :], jnp.sin(angles)[:, None, :]


def apply_rope(vectors, cos_tab, sin_tab):
    half_dim = vectors.shape[-1] // 2
    first_half = vectors[..., :half_dim]
    second_half = vectors[..., half_dim:]
    return jnp.concatenate([first_half * cos_tab - second_half * sin_tab, second_half * cos_tab + first_half * sin_tab], axis=-1)


def solution(mesh):
    tp_size = mesh.shape['tp']
    arg_specs = (P('dp', None), P('dp', None), P('dp'), P('tp', None), P(), P(), P(), P(), P(), P(), P(None, None, 'tp'), P(None, None, 'tp'), P(None, 'tp', None), P(), P(None, 'dp'), P(None, 'dp'))
    result_specs = (P('dp', None), P('dp', None), P(None, 'dp'), P(None, 'dp'))

    def decode_local(tokens, targets, start_pos, embed_table, layer_norms, w_q, w_k, w_v, qk_norms, w_o, w_gate, w_up, w_down, norm_final, k_cache, v_cache):
        batch_rows, num_steps = tokens.shape
        num_layers, embed_dim, num_heads, head_dim = w_q.shape
        kv_heads = w_k.shape[2]
        window = k_cache.shape[2]
        vocab_local = embed_table.shape[0]
        tp_rank = lax.axis_index('tp')
        vocab_start = tp_rank * vocab_local
        heads_local = max(1, num_heads // tp_size)
        row_split = max(1, tp_size // num_heads)
        rows_local = batch_rows // row_split
        head_start = (tp_rank // row_split) * heads_local
        row_start = (tp_rank % row_split) * rows_local
        group_size = num_heads // kv_heads
        kv_local = max(1, heads_local // group_size)
        kv_start = head_start // group_size
        score_scale = head_dim ** -0.5
        normalizer = jnp.array(embed_dim ** 0.5, dtype=jnp.float32).astype(jnp.bfloat16).astype(jnp.float32)
        row_ids = jnp.arange(batch_rows)
        slot_ids = jnp.arange(window)
        wq_local = [lax.dynamic_slice_in_dim(w_q[layer_idx], head_start, heads_local, axis=1) for layer_idx in range(num_layers)]
        wo_local = [lax.dynamic_slice_in_dim(w_o[layer_idx], head_start, heads_local, axis=0) for layer_idx in range(num_layers)]
        logprobs = []
        log_norms = []
        for step_idx in range(num_steps):
            positions = start_pos + step_idx
            slot_now = positions % window
            slot_valid = (positions[:, None] - (positions[:, None] - slot_ids[None, :]) % window) >= 0
            valid_rows = lax.dynamic_slice_in_dim(slot_valid, row_start, rows_local, axis=0)
            cos_tab, sin_tab = rope_tables(positions, head_dim)
            cos_rows = lax.dynamic_slice_in_dim(cos_tab, row_start, rows_local, axis=0)
            sin_rows = lax.dynamic_slice_in_dim(sin_tab, row_start, rows_local, axis=0)
            tok_local = tokens[:, step_idx] - vocab_start
            tok_here = (tok_local >= 0) & (tok_local < vocab_local)
            tok_rows = jnp.take(embed_table, jnp.clip(tok_local, 0, vocab_local - 1), axis=0)
            hidden = lax.psum(jnp.where(tok_here[:, None], tok_rows.astype(jnp.float32), 0.0), 'tp') * normalizer
            for layer_idx in range(num_layers):
                normed = rms_norm(hidden, layer_norms[layer_idx, 0]).astype(jnp.bfloat16)
                keys_new = jnp.einsum('bd,dke->bke', normed, w_k[layer_idx], preferred_element_type=jnp.float32)
                keys_new = apply_rope(rms_norm(keys_new, qk_norms[layer_idx, 1]), cos_tab, sin_tab).astype(jnp.bfloat16)
                values_new = jnp.einsum('bd,dke->bke', normed, w_v[layer_idx], preferred_element_type=jnp.float32).astype(jnp.bfloat16)
                k_cache = k_cache.at[layer_idx, row_ids, slot_now].set(keys_new)
                v_cache = v_cache.at[layer_idx, row_ids, slot_now].set(values_new)
                normed_rows = lax.dynamic_slice_in_dim(normed, row_start, rows_local, axis=0)
                query_rows = jnp.einsum('bd,dhe->bhe', normed_rows, wq_local[layer_idx], preferred_element_type=jnp.float32)
                query_rows = apply_rope(rms_norm(query_rows, qk_norms[layer_idx, 0]), cos_rows, sin_rows).astype(jnp.bfloat16)
                query_rows = query_rows.reshape(rows_local, kv_local, heads_local // kv_local, head_dim)
                keys_rows = lax.dynamic_slice(k_cache, (layer_idx, row_start, 0, kv_start, 0), (1, rows_local, window, kv_local, head_dim))[0]
                vals_rows = lax.dynamic_slice(v_cache, (layer_idx, row_start, 0, kv_start, 0), (1, rows_local, window, kv_local, head_dim))[0]
                scores = jnp.einsum('bkge,bske->bkgs', query_rows, keys_rows, preferred_element_type=jnp.float32) * score_scale
                scores = jnp.where(valid_rows[:, None, None, :], scores, -1e30)
                attn_probs = jax.nn.softmax(scores, axis=-1).astype(jnp.bfloat16)
                attn_heads = jnp.einsum('bkgs,bske->bkge', attn_probs, vals_rows, preferred_element_type=jnp.float32).astype(jnp.bfloat16)
                attn_heads = attn_heads.reshape(rows_local, heads_local, head_dim)
                attn_part = jnp.einsum('bhe,hed->bd', attn_heads, wo_local[layer_idx], preferred_element_type=jnp.float32)
                if row_split > 1:
                    attn_part = lax.dynamic_update_slice_in_dim(jnp.zeros((batch_rows, embed_dim), jnp.float32), attn_part, row_start, axis=0)
                hidden = hidden + rms_norm(lax.psum(attn_part, 'tp'), layer_norms[layer_idx, 1])
                mlp_in = rms_norm(hidden, layer_norms[layer_idx, 2]).astype(jnp.bfloat16)
                gate_proj = jnp.dot(mlp_in, w_gate[layer_idx], preferred_element_type=jnp.float32)
                up_proj = jnp.dot(mlp_in, w_up[layer_idx], preferred_element_type=jnp.float32)
                mlp_act = (jax.nn.gelu(gate_proj, approximate=True) * up_proj).astype(jnp.bfloat16)
                down_part = jnp.dot(mlp_act, w_down[layer_idx], preferred_element_type=jnp.float32)
                hidden = hidden + rms_norm(lax.psum(down_part, 'tp'), layer_norms[layer_idx, 3])
            final_normed = rms_norm(hidden, norm_final).astype(jnp.bfloat16)
            logits = jnp.einsum('bd,vd->bv', final_normed, embed_table, preferred_element_type=jnp.float32)
            top_logit = lax.pmax(jnp.max(logits, axis=-1), 'tp')
            exp_sum = jnp.sum(jnp.exp(logits - top_logit[:, None]), axis=-1)
            tgt_local = targets[:, step_idx] - vocab_start
            tgt_here = (tgt_local >= 0) & (tgt_local < vocab_local)
            tgt_logit = jnp.take_along_axis(logits, jnp.clip(tgt_local, 0, vocab_local - 1)[:, None], axis=1)[:, 0]
            totals = lax.psum(jnp.stack([exp_sum, jnp.where(tgt_here, tgt_logit, 0.0)]), 'tp')
            log_z = top_logit + jnp.log(totals[0])
            logprobs.append(totals[1] - log_z)
            log_norms.append(log_z)
        return jnp.stack(logprobs, axis=1), jnp.stack(log_norms, axis=1), k_cache, v_cache

    return jax.shard_map(decode_local, mesh=mesh, in_specs=arg_specs, out_specs=result_specs, check_vma=False)
```

profile of v0, /device:TPU:0, one launch (start us, length us, event | category | flops | bytes accessed | tf_op | source)
XLA Modules:
  0.0 1158.0 jit_solution(11918385521495736224)
XLA Ops:
  7.2 33.4 %copy.179 = bf16[2,96,512,1,256]{4,2,3,1,0:T(8,128)(2,1)} copy(bf16[2,96,512,1,256]{4,2,3,1,0:T(8,128)(2,1)} %param.34) | data formatting | bytes 100663296
  40.7 33.5 %copy.180 = bf16[2,96,512,1,256]{4,2,3,1,0:T(8,128)(2,1)} copy(bf16[2,96,512,1,256]{4,2,3,1,0:T(8,128)(2,1)} %param.35) | data formatting | bytes 100663296
  75.3 5.5 gather_fusion
  84.2 6.4 gather_fusion.2
  90.6 4.7 fusion.423
  95.2 4.2 fusion.424
  103.3 9.3 all-reduce.16.cloned.1.call-done
  122.4 11.2 scatter_fusion
  133.6 11.6 fusion.11
  146.0 11.3 scatter_fusion.1
  157.3 10.0 fusion.10
  169.6 28.2 %all-reduce.18.cloned.1.call-done = f32[96,1152]{1,0:T(8,128)} async-done(((f32[96,1152]{1,0:T(8,128)}), f32[96,1152]{1,0:T(8,128)}) %all-reduce.18.cloned.1.call-update) | async-done | bytes 442384 | tf_op jit(solution)/shard_map/psum | solution.py:92
  200.3 4.3 fusion.108
  204.6 6.4 fusion.34
  211.1 5.5 gather_fusion.4
  216.6 26.7 %all-reduce.32.cloned.1.call-done = (f32[96,1152]{1,0:T(8,128)}, f32[96,1152]{1,0:T(8,128)}) async-done(((f32[96,1152]{1,0:T(8,128)}, f32[96,1152]{1,0:T(8,128)}), (f32[96,1152]{1,0:T(8,128)}, f32[96,1152]{1,0:T(8,128)})) %all-reduce.32.cloned.1.call-update) | async-done | bytes 884752 | tf_op jit(solution)/shard_map/psum | solution.py:98
  257.0 11.2 scatter_fusion.3
  268.8 11.2 scatter_fusion.2
  280.0 33.4 %copy.159 = bf16[2,96,512,256]{3,2,1,0:T(8,128)(2,1)} copy(bf16[2,96,512,256]{3,2,1,0:T(8,128)(2,1)} %scatter_fusion.2) | data formatting | bytes 100663296
  313.4 11.2 scatter_fusion.4
  324.6 11.5 fusion.7
  336.9 33.4 %copy.157 = bf16[2,96,512,256]{3,2,1,0:T(8,128)(2,1)} copy(bf16[2,96,512,256]{3,2,1,0:T(8,128)(2,1)} %scatter_fusion.3) | data formatting | bytes 100663296
  370.3 11.2 scatter_fusion.5
  381.5 10.0 fusion.6
  397.3 24.3 %all-reduce.20.cloned.1.call-done = f32[96,1152]{1,0:T(8,128)} async-done(((f32[96,1152]{1,0:T(8,128)}), f32[96,1152]{1,0:T(8,128)}) %all-reduce.20.cloned.1.call-update) | async-done | bytes 442384 | tf_op jit(solution)/shard_map/psum | solution.py:92
  424.0 4.3 fusion.126
  428.4 6.4 fusion.32
  436.5 30.6 %all-reduce.30.cloned.1.call-done = (f32[96,1152]{1,0:T(8,128)}, f32[96,1152]{1,0:T(8,128)}) async-done(((f32[96,1152]{1,0:T(8,128)}, f32[96,1152]{1,0:T(8,128)}), (f32[96,1152]{1,0:T(8,128)}, f32[96,1152]{1,0:T(8,128)})) %all-reduce.30.cloned.1.call-update) | async-done | bytes 884752 | tf_op jit(solution)/shard_map/psum | solution.py:98
  479.3 11.1 scatter_fusion.7
  491.0 11.2 scatter_fusion.6
  502.2 33.4 %copy.166 = bf16[2,96,512,256]{3,2,1,0:T(8,128)(2,1)} copy(bf16[2,96,512,256]{3,2,1,0:T(8,128)(2,1)} %scatter_fusion.6) | data formatting | bytes 100663296
  535.7 11.8 %scatter_fusion.8 = bf16[2,96,512,256]{3,2,1,0:T(8,128)(2,1)} fusion(bf16[2,96,512,256]{3,2,1,0:T(8,128)(2,1)} %copy.166, s32[96]{0:T(128)S(1)} %copy-done.1, bf16[96,256]{1,0:T(8,128)(2,1)S(1)} %maximum_bitcast_fusion.9), kind=kCustom, calls=%fused_computation.14 | custom fusion | bytes 148608 | tf_op jit(solution)/shard_map/scatter | solution.py:76
  547.5 11.5 fusion.3
  559.8 33.4 %copy.164 = bf16[2,96,512,256]{3,2,1,0:T(8,128)(2,1)} copy(bf16[2,96,512,256]{3,2,1,0:T(8,128)(2,1)} %scatter_fusion.7) | data formatting | bytes 100663296
  593.2 11.8 %scatter_fusion.9 = bf16[2,96,512,256]{3,2,1,0:T(8,128)(2,1)} fusion(bf16[2,96,512,256]{3,2,1,0:T(8,128)(2,1)} %copy.164, s32[96]{0:T(128)S(1)} %copy-done.1, bf16[96,256]{1,0:T(8,128)(2,1)S(1)} %convolution_convert_fusion.1), kind=kCustom, calls=%fused_computation.15 | custom fusion | bytes 148608 | tf_op jit(solution)/shard_map/scatter | solution.py:77
  605.0 10.0 fusion.2
  617.9 27.2 %all-reduce.22.cloned.1.call-done = f32[96,1152]{1,0:T(8,128)} async-done(((f32[96,1152]{1,0:T(8,128)}), f32[96,1152]{1,0:T(8,128)}) %all-reduce.22.cloned.1.call-update) | async-done | bytes 442384 | tf_op jit(solution)/shard_map/psum | solution.py:92
  647.6 3.4 fusion.144
  651.0 6.2 fusion.30
  657.3 29.3 %all-reduce.24.cloned.1.call-done = f32[96,1152]{1,0:T(8,128)} async-done(((f32[96,1152]{1,0:T(8,128)}), f32[96,1152]{1,0:T(8,128)}) %all-reduce.24.cloned.1.call-update) | async-done | bytes 442384 | tf_op jit(solution)/shard_map/psum | solution.py:98
  692.7 11.5 fusion.5
  705.1 10.0 fusion.4
  715.1 11.8 %scatter_fusion.11 = bf16[2,96,512,256]{3,2,1,0:T(8,128)(2,1)} fusion(bf16[2,96,512,256]{3,2,1,0:T(8,128)(2,1)} %scatter_fusion.9, s32[96]{0:T(128)S(1)} %copy-done, bf16[96,256]{1,0:T(8,128)(2,1)S(1)} %convolution_convert_fusion), kind=kCustom, calls=%fused_computation.17 | custom fusion | bytes 148608 | tf_op jit(solution)/shard_map/scatter | solution.py:77
  727.4 11.8 %scatter_fusion.10 = bf16[2,96,512,256]{3,2,1,0:T(8,128)(2,1)} fusion(bf16[2,96,512,256]{3,2,1,0:T(8,128)(2,1)} %scatter_fusion.8, s32[96]{0:T(128)S(1)} %copy-done, bf16[96,256]{1,0:T(8,128)(2,1)S(1)} %maximum_bitcast_fusion.11), kind=kCustom, calls=%fused_computation.16 | custom fusion | bytes 148608 | tf_op jit(solution)/shard_map/scatter | solution.py:76
  739.2 11.5 fusion.9
  751.5 10.0 fusion.8
  761.5 11.5 fusion.1
  773.9 10.3 fusion
  787.4 36.3 %all-reduce.28.cloned.1.call-done = (f32[96,1152]{1,0:T(8,128)}, f32[96,1152]{1,0:T(8,128)}, f32[96,1152]{1,0:T(8,128)}) async-done(((f32[96,1152]{1,0:T(8,128)}, f32[96,1152]{1,0:T(8,128)}, f32[96,1152]{1,0:T(8,128)}), (f32[96,1152]{1,0:T(8,128)}, f32[96,1152]{1,0:T(8,128)}, f32[96,1152]{1,0:T(8,128)})) %all-reduce.28.cloned.1.call-update) | async-done | bytes 1327120 | tf_op jit(solution)/shard_map/psum | solution.py:92
  829.0 3.4 fusion.117
  832.4 6.2 fusion.16
  838.6 3.4 fusion.135
  842.0 6.2 fusion.14
  848.2 3.4 fusion.153
  851.7 6.2 fusion.12
  859.0 35.0 %all-reduce.26.cloned.1.call-done = (f32[96,1152]{1,0:T(8,128)}, f32[96,1152]{1,0:T(8,128)}, f32[96,1152]{1,0:T(8,128)}) async-done(((f32[96,1152]{1,0:T(8,128)}, f32[96,1152]{1,0:T(8,128)}, f32[96,1152]{1,0:T(8,128)}), (f32[96,1152]{1,0:T(8,128)}, f32[96,1152]{1,0:T(8,128)}, f32[96,1152]{1,0:T(8,128)})) %all-reduce.26.cloned.1.call-update) | async-done | bytes 1327120 | tf_op jit(solution)/shard_map/psum | solution.py:98
  899.3 63.6 %fusion.425 = (f32[96]{0:T(128)S(1)}, f32[96,65536]{1,0:T(8,128)}) fusion(bf16[65536,1152]{1,0:T(8,128)(2,1)} %param.23, f32[96]{0:T(128)S(1)} %add_rsqrt_fusion, f32[1152]{0:T(1024)S(1)} %broadcast_add_fusion, f32[96,1152]{1,0:T(8,128)S(1)} %get-tuple-element.34, f32[1152]{0:T(1024)S(1)} %copy-done.20, f32[96,1152]{1,0:T(8,128)} %get-tuple-element.22, ...), kind=kOutput, calls=%fused_computation.684 | convolution fusion | flops 14502469632 | bytes 177055872 | tf_op jit(solution)/shard_map/bd,vd->bv/dot_general | solution.py:100
  962.9 67.3 %fusion.426 = (f32[96]{0:T(128)S(1)}, f32[96,65536]{1,0:T(8,128)}) fusion(bf16[65536,1152]{1,0:T(8,128)(2,1)} %param.23, f32[96]{0:T(128)S(1)} %add_rsqrt_fusion.12, f32[1152]{0:T(1024)S(1)} %broadcast_add_fusion, f32[96,1152]{1,0:T(8,128)S(1)} %get-tuple-element.86, f32[1152]{0:T(1024)S(1)} %copy-done.20, f32[96,1152]{1,0:T(8,128)S(1)} %copy-done.14, ...), kind=kOutput, calls=%fused_computation.685 | convolution fusion | flops 14502469632 | bytes 177055872 | tf_op jit(solution)/shard_map/bd,vd->bv/dot_general | solution.py:100
  1030.2 67.3 %fusion.427 = (f32[96]{0:T(128)S(1)}, f32[96,65536]{1,0:T(8,128)}) fusion(bf16[65536,1152]{1,0:T(8,128)(2,1)} %param.23, f32[1152]{0:T(1024)S(1)} %broadcast_add_fusion, f32[96]{0:T(128)S(1)} %add_rsqrt_fusion.24, f32[96,1152]{1,0:T(8,128)S(1)} %get-tuple-element.88, f32[1152]{0:T(1024)S(1)} %copy-done.20, f32[96,1152]{1,0:T(8,128)S(1)} %copy-done.13, ...), kind=kOutput, calls=%fused_computation.686 | convolution fusion | flops 14502469632 | bytes 177055872 | tf_op jit(solution)/shard_map/bd,vd->bv/dot_general | solution.py:100
  1100.8 5.8 all-reduce.5
  1106.6 10.3 exponential_reduce_fusion.2
  1120.1 10.3 exponential_reduce_fusion.1
  1133.8 10.3 exponential_reduce_fusion
  1144.2 5.7 all-reduce
  (297 shorter events, 102.0 us)
Async XLA Ops:
  7.2 105.4 %all-reduce.16.cloned.1.call-start = ((), (), s32[]{:S(2)}) async-start(), calls=%async_computation | async-start | bytes 884736 | tf_op jit(solution)/shard_map/psum | solution.py:70
  40.6 33.5 %copy-start.44 = (s32[96,3]{0,1:T(4,128)S(1)}, s32[96,3]{0,1:T(4,128)}, u32[]{:S(2)}) copy-start(s32[96,3]{0,1:T(4,128)} %param.20) | copy-start | bytes 3460
  40.6 41.7 %copy-start.27 = (s32[96]{0:T(128)S(1)}, s32[96]{0:T(128)}, u32[]{:S(2)}) copy-start(s32[96]{0:T(128)} %param.22) | copy-start | bytes 1156
  40.6 42.3 %copy-start.49 = (f32[2,2,256]{2,1,0:T(2,128)S(1)}, f32[2,2,256]{2,1,0:T(2,128)}, u32[]{:S(2)}) copy-start(f32[2,2,256]{2,1,0:T(2,128)} %param.28) | copy-start | bytes 12292
  40.7 42.9 %copy-start.26 = (f32[2,4,1152]{2,1,0:T(4,128)S(1)}, f32[2,4,1152]{2,1,0:T(4,128)}, u32[]{:S(2)}) copy-start(f32[2,4,1152]{2,1,0:T(4,128)} %param.24) | copy-start | bytes 110596
  81.7 116.1 %all-reduce.18.cloned.1.call-start = ((), (), s32[]{:S(2)}) async-start(), calls=%async_computation.1 | async-start | bytes 884736 | tf_op jit(solution)/shard_map/psum | solution.py:92
  101.9 43.2 %copy-start.15 = (bf16[1,1152,1,256]{3,2,1,0:T(2,128)(2,1)}, bf16[1,1152,1,256]{3,2,1,0:T(2,128)(2,1)S(1)}, u32[]{:S(2)}) copy-start(bf16[1,1152,1,256]{3,2,1,0:T(2,128)(2,1)S(1)} %constant_dynamic-slice_fusion.1) | copy-start | bytes 1769476
  133.6 11.6 copy-start.28
  157.2 11.4 copy-start.17
  157.2 11.4 copy-start.53
  157.2 11.4 copy-start.54
  157.3 41.7 %copy-start.8 = (f32[96,1152]{1,0:T(8,128)S(1)}, f32[96,1152]{1,0:T(8,128)}, u32[]{:S(2)}) copy-start(f32[96,1152]{1,0:T(8,128)} %all-reduce.16.cloned.1.call-done) | copy-start | bytes 1327108
  157.3 41.7 %copy-start.23 = (f32[1152]{0:T(1024)S(1)}, f32[1152]{0:T(1024)}, u32[]{:S(2)}) copy-start(f32[1152]{0:T(1024)} %get-tuple-element.11) | copy-start | bytes 13828
  157.3 43.0 %copy-start.39 = (f32[1152]{0:T(1024)S(1)}, f32[1152]{0:T(1024)}, u32[]{:S(2)}) copy-start(f32[1152]{0:T(1024)} %get-tuple-element.10) | copy-start | bytes 13828
  168.4 74.9 %all-reduce.32.cloned.1.call-start = ((), (), s32[]{:S(2)}) async-start(), calls=%async_computation.8 | async-start | bytes 1769472 | tf_op jit(solution)/shard_map/psum | solution.py:98
  200.2 10.8 copy-start.50
  204.6 39.9 %copy-start.24 = (f32[1152]{0:T(1024)S(1)}, f32[1152]{0:T(1024)}, u32[]{:S(2)}) copy-start(f32[1152]{0:T(1024)} %get-tuple-element.12) | copy-start | bytes 13828
  204.6 47.2 %copy-start.22 = (f32[1152]{0:T(1024)S(1)}, f32[1152]{0:T(1024)}, u32[]{:S(2)}) copy-start(f32[1152]{0:T(1024)} %get-tuple-element.9) | copy-start | bytes 13828
  204.6 49.2 %copy-start.21 = (f32[1152]{0:T(1024)S(1)}, f32[1152]{0:T(1024)}, u32[]{:S(2)}) copy-start(f32[1152]{0:T(1024)} %get-tuple-element.8) | copy-start | bytes 13828
  211.0 45.8 %copy-start.36 = (f32[1,1,256]{2,1,0:T(1,128)S(1)}, f32[1,1,256]{2,1,0:T(1,128)}, u32[]{:S(2)}) copy-start(f32[1,1,256]{2,1,0:T(1,128)} %get-tuple-element.91) | copy-start | bytes 3076
  211.0 45.9 %copy-start.35 = (f32[1,1,256]{2,1,0:T(1,128)S(1)}, f32[1,1,256]{2,1,0:T(1,128)}, u32[]{:S(2)}) copy-start(f32[1,1,256]{2,1,0:T(1,128)} %get-tuple-element.90) | copy-start | bytes 3076
  211.0 57.2 %copy-start.34 = (f32[1,1,256]{2,1,0:T(1,128)S(1)}, f32[1,1,256]{2,1,0:T(1,128)}, u32[]{:S(2)}) copy-start(f32[1,1,256]{2,1,0:T(1,128)} %get-tuple-element.92) | copy-start | bytes 3076
  211.0 57.3 %copy-start.37 = (f32[128]{0:T(128)S(1)}, f32[128]{0:T(128)}, u32[]{:S(2)}) copy-start(f32[128]{0:T(128)} %multiply_power_fusion) | copy-start | bytes 1540
  211.0 57.3 %copy-start.41 = (f32[96]{0:T(128)S(1)}, f32[96]{0:T(128)}, u32[]{:S(2)}) copy-start(f32[96]{0:T(128)} %get-tuple-element.131) | copy-start | bytes 1156
  211.0 57.3 %copy-start.43 = (f32[96]{0:T(128)S(1)}, f32[96]{0:T(128)}, u32[]{:S(2)}) copy-start(f32[96]{0:T(128)} %get-tuple-element.130) | copy-start | bytes 1156
  211.0 210.5 %all-reduce.20.cloned.1.call-start = ((), (), s32[]{:S(2)}) async-start(), calls=%async_computation.2 | async-start | bytes 884736 | tf_op jit(solution)/shard_map/psum | solution.py:92
  253.0 0.8 copy-start.9
  253.9 2.9 copy-start.18
  324.6 11.5 copy-start.32
  336.9 33.4 %copy-start.25 = (bf16[96,256]{1,0:T(8,128)(2,1)S(1)}, bf16[96,256]{1,0:T(8,128)(2,1)}, u32[]{:S(2)}) copy-start(bf16[96,256]{1,0:T(8,128)(2,1)} %convolution_convert_fusion.3) | copy-start | bytes 147460
  381.5 11.5 copy-start.51
  381.5 11.6 copy-start.52
  381.5 41.2 %copy-start.7 = (f32[96,1152]{1,0:T(8,128)S(1)}, f32[96,1152]{1,0:T(8,128)}, u32[]{:S(2)}) copy-start(f32[96,1152]{1,0:T(8,128)} %get-tuple-element.29) | copy-start | bytes 1327108
  392.6 74.5 %all-reduce.30.cloned.1.call-start = ((), (), s32[]{:S(2)}) async-start(), calls=%async_computation.7 | async-start | bytes 1769472 | tf_op jit(solution)/shard_map/psum | solution.py:98
  424.0 10.8 copy-start.19
  434.8 55.8 %copy-start.47 = (f32[96]{0:T(128)S(1)}, f32[96]{0:T(128)}, u32[]{:S(2)}) copy-start(f32[96]{0:T(128)} %get-tuple-element.129) | copy-start | bytes 1156
  434.8 210.3 %all-reduce.22.cloned.1.call-start = ((), (), s32[]{:S(2)}) async-start(), calls=%async_computation.3 | async-start | bytes 884736 | tf_op jit(solution)/shard_map/psum | solution.py:92
  469.5 1.4 copy-start.11
  502.2 33.5 %copy-start.1 = (s32[96]{0:T(128)S(1)}, s32[96]{0:T(128)}, u32[]{:S(2)}) copy-start(s32[96]{0:T(128)} %get-tuple-element.136) | copy-start | bytes 1156
  547.5 11.5 copy-start.31
  605.0 41.3 %copy-start.6 = (f32[96,1152]{1,0:T(8,128)S(1)}, f32[96,1152]{1,0:T(8,128)}, u32[]{:S(2)}) copy-start(f32[96,1152]{1,0:T(8,128)} %get-tuple-element.27) | copy-start | bytes 1327108
  616.0 70.6 %all-reduce.24.cloned.1.call-start = ((), (), s32[]{:S(2)}) async-start(), calls=%async_computation.4 | async-start | bytes 884736 | tf_op jit(solution)/shard_map/psum | solution.py:98
  651.0 38.2 %copy-start.16 = (bf16[1,1152,1,256]{3,2,1,0:T(2,128)(2,1)S(1)}, bf16[1,1152,1,256]{3,2,1,0:T(2,128)(2,1)}, u32[]{:S(2)}) copy-start(bf16[1,1152,1,256]{3,2,1,0:T(2,128)(2,1)} %constant_dynamic-slice_fusion) | copy-start | bytes 1769476
  651.0 41.3 %copy-start.48 = (f32[1,1,256]{2,1,0:T(1,128)S(1)}, f32[1,1,256]{2,1,0:T(1,128)}, u32[]{:S(2)}) copy-start(f32[1,1,256]{2,1,0:T(1,128)} %get-tuple-element.89) | copy-start | bytes 3076
  657.3 166.4 %all-reduce.28.cloned.1.call-start = ((), (), s32[]{:S(2)}) async-start(), calls=%async_computation.6 | async-start | bytes 2654208 | tf_op jit(solution)/shard_map/psum | solution.py:92
  692.7 11.5 copy-start.33
  705.0 10.0 copy-start
  705.1 21.9 %copy-start.42 = (f32[96]{0:T(128)S(1)}, f32[96]{0:T(128)}, u32[]{:S(2)}) copy-start(f32[96]{0:T(128)} %get-tuple-element.131) | copy-start | bytes 1156
  739.2 11.5 copy-start.29
  773.8 10.4 copy-start.2
  773.8 13.5 %copy-start.45 = (s32[96,3]{0,1:T(4,128)S(1)}, s32[96,3]{0,1:T(4,128)}, u32[]{:S(2)}) copy-start(s32[96,3]{0,1:T(4,128)} %param.21) | copy-start | bytes 3460
  773.8 53.4 %copy-start.10 = (f32[96,1152]{1,0:T(8,128)S(1)}, f32[96,1152]{1,0:T(8,128)}, u32[]{:S(2)}) copy-start(f32[96,1152]{1,0:T(8,128)} %copy-done.9) | copy-start | bytes 1327108
  773.9 53.4 %copy-start.12 = (f32[96,1152]{1,0:T(8,128)S(1)}, f32[96,1152]{1,0:T(8,128)}, u32[]{:S(2)}) copy-start(f32[96,1152]{1,0:T(8,128)} %copy-done.11) | copy-start | bytes 1327108
  773.9 53.4 %copy-start.30 = (f32[1152]{0:T(1024)S(1)}, f32[1152]{0:T(1024)}, u32[]{:S(2)}) copy-start(f32[1152]{0:T(1024)} %get-tuple-element.7) | copy-start | bytes 13828
  784.2 44.8 %copy-start.38 = (f32[1152]{0:T(1024)S(1)}, f32[1152]{0:T(1024)}, u32[]{:S(2)}) copy-start(f32[1152]{0:T(1024)} %get-tuple-element.6) | copy-start | bytes 13828
  787.3 106.7 %all-reduce.26.cloned.1.call-start = ((), (), s32[]{:S(2)}) async-start(), calls=%async_computation.5 | async-start | bytes 2654208 | tf_op jit(solution)/shard_map/psum | solution.py:98
  848.2 10.7 copy-start.40
  851.7 45.9 %copy-start.20 = (f32[1152]{0:T(1024)S(1)}, f32[1152]{0:T(1024)}, u32[]{:S(2)}) copy-start(f32[1152]{0:T(1024)} %get-tuple-element.13) | copy-start | bytes 13828
  899.3 63.6 %copy-start.14 = (f32[96,1152]{1,0:T(8,128)S(1)}, f32[96,1152]{1,0:T(8,128)}, u32[]{:S(2)}) copy-start(f32[96,1152]{1,0:T(8,128)} %get-tuple-element.21) | copy-start | bytes 1327108
  962.9 67.3 %copy-start.13 = (f32[96,1152]{1,0:T(8,128)S(1)}, f32[96,1152]{1,0:T(8,128)}, u32[]{:S(2)}) copy-start(f32[96,1152]{1,0:T(8,128)} %get-tuple-element.20) | copy-start | bytes 1327108
  1030.2 67.3 %copy-start.5 = (s32[96]{0:T(128)S(1)}, s32[96]{0:T(128)}, u32[]{:S(2)}) copy-start(s32[96]{0:T(128)} %or_bitcast_fusion.2) | copy-start | bytes 1156
  1106.6 10.3 copy-start.4
  1120.1 10.3 copy-start.3
  1133.7 10.3 copy-start.46
Sparse Core Ops, SparseCore 0:
  81.8 30.7 all-reduce.15
  168.5 29.2 all-reduce.17
  211.2 32.1 all-reduce.31
  392.7 28.8 all-reduce.19
  434.9 32.0 all-reduce.29
  616.2 28.8 all-reduce.21
  657.4 29.1 all-reduce.23
  787.4 36.2 all-reduce.27
  858.0 35.9 all-reduce.25
where the time goes:
time: 1170 us; the launch traced here: 1160 us
  matrix products  418 us (36%)
  local copies, waits for them, and re-layouts  380 us (32%)
  waiting for transfers between devices  247 us (21%)
  other arithmetic  84.1 us (7%)
  between operations  15.9 us (1%)
    unnamed x116, local copies, waits for them, and re-layouts  202 us
    dot_general x3, matrix products, decode_local(): jnp.einsum('bd,vd->bv', final_normed, embed_table, preferred_element_type...  198 us
    psum x4, waiting for transfers between devices, decode_local(): lax.psum(down_part, 'tp')  122 us
    psum x4, waiting for transfers between devices, decode_local(): lax.psum(attn_part, 'tp')  116 us
    dot_general x6, matrix products, decode_local(): jnp.einsum('bkge,bske->bkgs', query_rows, keys_rows, preferred_element_ty...  69 us
    scatter x6, local copies, waits for them, and re-layouts, decode_local(): k_cache = k_cache.at[layer_idx, row_ids, slot_now].set(keys_new)  68.4 us
    scatter x6, local copies, waits for them, and re-layouts, decode_local(): v_cache = v_cache.at[layer_idx, row_ids, slot_now].set(values_new)  68.3 us
    dot_general x6, matrix products, decode_local(): jnp.einsum('bkgs,bske->bkge', attn_probs, vals_rows, preferred_element_ty...  60.4 us
  transfers between devices with their start and end apart: 9, of which 9 were waited for; matrix products, arithmetic and copies ran while one was open for 3% of the time, Pallas kernels for 0%

commit v1 on v0

v1 whole, which is shorter than its diff:
```python
import functools

import jax
import jax.numpy as jnp
import numpy as np
from jax import lax
from jax.experimental import pallas as pl
from jax.experimental.pallas import tpu as pltpu
from jax.sharding import PartitionSpec as P

EPSILON = 1e-6
ROPE_BASE = 10000.0
NEG = -1e30
MESH = pl.DeviceIdType.MESH
F32 = jnp.float32
BF16 = jnp.bfloat16
NT = (((1,), (1,)), ((), ()))
VMEM_LIMIT = 62 * 1024 * 1024


def rms(values, weight):
    mean_sq = jnp.mean(values * values, axis=-1, keepdims=True)
    return values * lax.rsqrt(mean_sq + EPSILON) * (1.0 + weight)


def vspec():
    return pl.BlockSpec(memory_space=pltpu.VMEM)


def aspec():
    return pl.BlockSpec(memory_space=pl.ANY)


def sspec():
    return pl.BlockSpec(memory_space=pltpu.SMEM)


def gather_kernel(rows, grp_ref, col_ref, table_ref, out_ref, xbuf, sem):
    def issue(i, carry):
        src = pl.multiple_of(grp_ref[i] * 8, 8)
        dst = pl.multiple_of(i * 8, 8)
        pltpu.make_async_copy(table_ref.at[pl.ds(src, 8), :], xbuf.at[pl.ds(dst, 8), :], sem).start()
        return carry

    lax.fori_loop(0, rows, issue, 0)
    pltpu.make_async_copy(table_ref.at[pl.ds(0, rows * 8), :], xbuf, sem).wait()
    for c in range(rows // 32):
        lanes = lax.broadcasted_iota(jnp.int32, (32, 256), 1)
        pick = jnp.where(lanes == col_ref[c * 32:(c + 1) * 32, :], 1.0, 0.0).astype(BF16)
        out_ref[c * 32:(c + 1) * 32, :] = jnp.dot(pick, xbuf[c * 256:(c + 1) * 256, :], preferred_element_type=F32)


def gather_rows(ids, table):
    rows = ids.shape[0]
    vocab_local, dim = table.shape
    here = (ids >= 0) & (ids < vocab_local)
    safe = jnp.clip(ids, 0, vocab_local - 1)
    col = jnp.where(here, (jnp.arange(rows) % 32) * 8 + safe % 8, -1)[:, None]
    return pl.pallas_call(
        functools.partial(gather_kernel, rows),
        out_shape=jax.ShapeDtypeStruct((rows, dim), F32),
        in_specs=[sspec(), vspec(), aspec()],
        out_specs=vspec(),
        scratch_shapes=[pltpu.VMEM((rows * 8, dim), BF16), pltpu.SemaphoreType.DMA],
        compiler_params=pltpu.CompilerParams(vmem_limit_bytes=24 * 1024 * 1024),
        name="token_rows",
    )(safe // 8, col, table)


def sum_kernel(rows, chunks, part_ref, out_ref, got1, half, got2, total, got3, s1, r1, s2, r2, s3, r3):
    dp = lax.axis_index("dp")
    tp = lax.axis_index("tp")
    core = lax.rem(tp, 2)
    mate = (dp, tp + 1 - 2 * core)
    across = (dp, lax.rem(tp + 2, 4))
    barrier = pltpu.get_barrier_semaphore()
    for peer in (mate, across):
        pl.semaphore_signal(barrier, inc=1, device_id=peer, device_id_type=MESH)
    pl.semaphore_wait(barrier, 2)
    hrows = rows // 2
    crows = hrows // chunks
    own = core * hrows
    other = (1 - core) * hrows

    def send(src, dst, ssem, rsem, peer):
        return pltpu.make_async_remote_copy(src_ref=src, dst_ref=dst, send_sem=ssem, recv_sem=rsem, device_id=peer, device_id_type=MESH)

    first, second, third = [], [], []
    for j in range(chunks):
        at = pl.multiple_of(other + j * crows, 8)
        first.append(send(part_ref.at[pl.ds(at, crows), :], got1.at[j], s1.at[j], r1.at[j], mate))
        first[-1].start()
    for j in range(chunks):
        first[j].wait_recv()
        at = pl.multiple_of(own + j * crows, 8)
        half[j] = part_ref[pl.ds(at, crows), :] + got1[j]
        second.append(send(half.at[j], got2.at[j], s2.at[j], r2.at[j], across))
        second[-1].start()
    for j in range(chunks):
        second[j].wait_recv()
        at = pl.multiple_of(own + j * crows, 8)
        value = half[j] + got2[j]
        total[j] = value
        out_ref[pl.ds(at, crows), :] = value
        third.append(send(total.at[j], got3.at[j], s3.at[j], r3.at[j], mate))
        third[-1].start()
    for j in range(chunks):
        third[j].wait_recv()
        at = pl.multiple_of(other + j * crows, 8)
        out_ref[pl.ds(at, crows), :] = got3[j]
    for j in range(chunks):
        first[j].wait_send()
        second[j].wait_send()
        third[j].wait_send()


def sum_tp(part, cid):
    rows, dim = part.shape
    chunks = 3
    buf = pltpu.VMEM((chunks, rows // 2 // chunks, dim), F32)
    sems = pltpu.SemaphoreType.DMA((chunks,))
    return pl.pallas_call(
        functools.partial(sum_kernel, rows, chunks),
        out_shape=jax.ShapeDtypeStruct((rows, dim), F32),
        in_specs=[vspec()],
        out_specs=vspec(),
        scratch_shapes=[buf] * 5 + [sems] * 6,
        compiler_params=pltpu.CompilerParams(collective_id=cid, has_side_effects=True, vmem_limit_bytes=24 * 1024 * 1024),
        name="sum_tp",
    )(part)


NB = 8
NBUF = 4


def layer_kernel(layer, batch, steps, normalizer, *refs):
    if layer == 0:
        (start_ref, startv_ref, cos_ref, sin_ref, ln_ref, qk_ref, ar_ref,
         wq_hbm, wk_hbm, wv_hbm, wo_hbm, wg_hbm, wu_hbm, wd_hbm, k_hbm, v_hbm,
         hid_ref, part_ref, ko_hbm, vo_hbm, *scratch) = refs
        prev_ref = None
    else:
        (start_ref, startv_ref, cos_ref, sin_ref, ln_ref, qk_ref, ar_ref, prev_ref,
         wq_hbm, wk_hbm, wv_hbm, wo_hbm, wg_hbm, wu_hbm, wd_hbm, k_hbm, v_hbm, _, _,
         hid_ref, part_ref, ko_hbm, vo_hbm, *scratch) = refs
    wq, wk, wv, wo, wg, wu, wd, kbuf, vbuf, qs, kn, vn, os, wsem, rsem, osem = scratch
    heads = 4
    nblk = batch // NB
    rows = batch * steps
    ln = lambda l, j: ln_ref[4 * l + j:4 * l + j + 1, :]

    weights = [(wq_hbm, wq), (wk_hbm, wk), (wv_hbm, wv), (wo_hbm, wo), (wg_hbm, wg), (wu_hbm, wu), (wd_hbm, wd)]
    wcopies = [pltpu.make_async_copy(src.at[layer], dst, wsem.at[n]) for n, (src, dst) in enumerate(weights)]

    def reads(i, slot):
        at = pl.ds(pl.multiple_of(i * NB, NB), NB)
        return (pltpu.make_async_copy(k_hbm.at[layer, at], kbuf.at[slot], rsem.at[0, slot]),
                pltpu.make_async_copy(v_hbm.at[layer, at], vbuf.at[slot], rsem.at[1, slot]))

    def writes(i, slot):
        at = pl.ds(pl.multiple_of(i * NB, NB), NB)
        return (pltpu.make_async_copy(kbuf.at[slot], ko_hbm.at[layer, at], osem.at[0, slot]),
                pltpu.make_async_copy(vbuf.at[slot], vo_hbm.at[layer, at], osem.at[1, slot]))

    for c in wcopies[:3]:
        c.start()
    for i in range(2):
        for c in reads(i, i):
            c.start()
    for c in wcopies[3:]:
        c.start()

    if layer == 0:
        hid = ar_ref[...] * normalizer
    else:
        hid = prev_ref[...] + rms(ar_ref[...], ln(layer - 1, 3))
    hid_ref[...] = hid
    act = rms(hid, ln(layer, 0)).astype(BF16)
    qs[...] = jnp.zeros_like(qs)
    kn[...] = jnp.zeros_like(kn)
    vn[...] = jnp.zeros_like(vn)
    for c in wcopies[:3]:
        c.wait()

    def put(dst, j, values, lane):
        for t in range(steps):
            dst[lane, pl.ds(t * j[0] + j[1], batch, stride=16), :] = values[t * batch:(t + 1) * batch, :]

    def wide(ref, at):
        return jnp.concatenate([ref[0, at, :], ref[1, at, :]], axis=1)

    def roped(x, weight):
        x = rms(x, weight)
        a, b = x[:, :128], x[:, 128:]
        c, s = cos_ref[...], sin_ref[...]
        return a * c - b * s, b * c + a * s

    for h in range(heads):
        q = jnp.dot(act, wq[:, h * 256:(h + 1) * 256], preferred_element_type=F32)
        lo, hi = roped(q, qk_ref[2 * layer:2 * layer + 1, :])
        put(qs, (heads, h), lo, 0)
        put(qs, (heads, h), hi, 1)
    k = jnp.dot(act, wk[...], preferred_element_type=F32)
    lo, hi = roped(k, qk_ref[2 * layer + 1:2 * layer + 2, :])
    put(kn, (1, 0), lo, 0)
    put(kn, (1, 0), hi, 1)
    v = jnp.dot(act, wv[...], preferred_element_type=F32)
    put(vn, (1, 0), v[:, :128], 0)
    put(vn, (1, 0), v[:, 128:], 1)

    scale = 256 ** -0.5
    m_rows = NB * 16

    def block(i, carry):
        slot = lax.rem(i, NBUF)
        for c in reads(i, slot):
            c.wait()

        @pl.when(i >= 1)
        def _():
            for c in writes(i - 1, lax.rem(i + NBUF - 1, NBUF)):
                c.start()

        @pl.when(i >= 2)
        def _():
            for c in writes(i - 2, lax.rem(i + NBUF - 2, NBUF)):
                c.wait()

        @pl.when(i + 2 < nblk)
        def _():
            for c in reads(i + 2, lax.rem(i + 2, NBUF)):
                c.start()

        r0 = pl.multiple_of(i * m_rows, m_rows)
        at = pl.ds(r0, m_rows)
        qb = wide(qs, at).astype(BF16)
        knf = wide(kn, at)
        vnf = wide(vn, at)
        start = startv_ref[at, :]
        row = lax.broadcasted_iota(jnp.int32, (m_rows, 128), 0)
        lane = lax.broadcasted_iota(jnp.int32, (m_rows, 128), 1)
        t = lax.shift_right_logical(row & 15, 2)
        old = jnp.concatenate([lax.dot_general(qb[16 * j:16 * j + 16, :], kbuf[slot, j], NT, preferred_element_type=F32) for j in range(NB)], axis=0) * scale
        new = lax.dot_general(qb, knf.astype(BF16), NT, preferred_element_type=F32) * scale
        cols = []
        for g in range(4):
            s = lane + 128 * g
            ok = (s <= start + t) & (((s - start) & 511) > t)
            cols.append(jnp.where(ok, old[:, 128 * g:128 * (g + 1)], NEG))
        ok = (lax.shift_right_logical(row, 4) == lax.shift_right_logical(lane, 4)) & ((lane & 15) <= t)
        cols.append(jnp.where(ok, new, NEG))
        top = jnp.maximum(jnp.maximum(jnp.maximum(cols[0], cols[1]), jnp.maximum(cols[2], cols[3])), cols[4])
        top = jnp.max(top, axis=-1, keepdims=True)
        exps = [jnp.exp(c - top) for c in cols]
        tot = jnp.sum((exps[0] + exps[1]) + (exps[2] + exps[3]) + exps[4], axis=-1, keepdims=True)
        inv = 1.0 / tot
        pold = jnp.concatenate([(e * inv).astype(BF16) for e in exps[:4]], axis=1)
        pnew = (exps[4] * inv).astype(BF16)
        out = jnp.dot(pnew, vnf.astype(BF16), preferred_element_type=F32)
        out = out + jnp.concatenate([jnp.dot(pold[16 * j:16 * j + 16, :], vbuf[slot, j], preferred_element_type=F32) for j in range(NB)], axis=0)
        os[0, at, :] = out[:, :128]
        os[1, at, :] = out[:, 128:]

        sub = lax.broadcasted_iota(jnp.int32, (16, 256), 0)
        for half in range(2):
            pending = []
            for j in range(half * NB // 2, (half + 1) * NB // 2):
                st = start_ref[i * NB + j]
                for w in (st & 511, (st + 2) & 511):
                    w = pl.multiple_of(lax.shift_left(lax.shift_right_logical(w, 4), 4), 16)
                    dist = (sub + w - st) & 511
                    for buf, fresh in ((kbuf, knf), (vbuf, vnf)):
                        value = buf[slot, j, pl.ds(w, 16), :].astype(F32)
                        for tt in range(steps):
                            value = jnp.where(dist == tt, fresh[16 * j + tt:16 * j + tt + 1, :], value)
                        pending.append((buf, j, w, value.astype(BF16)))
            for buf, j, w, value in pending:
                buf[slot, j, pl.ds(w, 16), :] = value
        return carry

    lax.fori_loop(0, nblk, block, 0)
    for c in writes(nblk - 1, (nblk - 1) % NBUF):
        c.start()

    wcopies[3].wait()
    attn = None
    for h in range(heads):
        parts = []
        for t in range(steps):
            parts.append(jnp.concatenate([os[g, pl.ds(t * heads + h, batch, stride=16), :] for g in range(2)], axis=1))
        x = jnp.concatenate(parts, axis=0).astype(BF16)
        y = jnp.dot(x, wo[h * 256:(h + 1) * 256, :], preferred_element_type=F32)
        attn = y if attn is None else attn + y
    hid = hid_ref[...] + rms(attn, ln(layer, 1))
    hid_ref[...] = hid
    act = rms(hid, ln(layer, 2)).astype(BF16)
    for c in wcopies[4:]:
        c.wait()
    width = wg.shape[0]
    for at in range(0, width, 512):
        n = min(512, width - at)
        gate = lax.dot_general(act, wg[at:at + n, :], NT, preferred_element_type=F32)
        up = lax.dot_general(act, wu[at:at + n, :], NT, preferred_element_type=F32)
        inner = (jax.nn.gelu(gate, approximate=True) * up).astype(BF16)
        down = jnp.dot(inner, wd[at:at + n, :], preferred_element_type=F32)
        if at == 0:
            part_ref[...] = down
        else:
            part_ref[...] += down
    for i in (nblk - 2, nblk - 1):
        for c in writes(i, i % NBUF):
            c.wait()


def run_layer(layer, small, ar, prev, weights, caches, outs):
    batch = small[0].shape[0]
    rows, dim = ar.shape
    steps = rows // batch
    normalizer = float(np.float32(dim ** 0.5).astype(BF16))
    kc, vc = caches
    width = weights[4].shape[1]
    ins = list(small) + [ar] + ([] if prev is None else [prev]) + list(weights) + [kc, vc]
    specs = [sspec()] + [vspec()] * (len(small) - 1) + [vspec()] * (1 if prev is None else 2) + [aspec()] * 9
    alias = {}
    if outs is not None:
        alias = {len(ins): 2, len(ins) + 1: 3}
        ins += list(outs)
        specs += [aspec()] * 2
    scratch = [
        pltpu.VMEM((dim, 1024), BF16), pltpu.VMEM((dim, 256), BF16), pltpu.VMEM((dim, 256), BF16),
        pltpu.VMEM((1024, dim), BF16), pltpu.VMEM((width, dim), BF16), pltpu.VMEM((width, dim), BF16), pltpu.VMEM((width, dim), BF16),
        pltpu.VMEM((NBUF, NB, 512, 256), BF16), pltpu.VMEM((NBUF, NB, 512, 256), BF16),
        pltpu.VMEM((2, batch * 16, 128), F32), pltpu.VMEM((2, batch * 16, 128), F32), pltpu.VMEM((2, batch * 16, 128), F32), pltpu.VMEM((2, batch * 16, 128), F32),
        pltpu.SemaphoreType.DMA((7,)), pltpu.SemaphoreType.DMA((2, NBUF)), pltpu.SemaphoreType.DMA((2, NBUF)),
    ]
    return pl.pallas_call(
        functools.partial(layer_kernel, layer, batch, steps, normalizer),
        out_shape=[jax.ShapeDtypeStruct((rows, dim), F32), jax.ShapeDtypeStruct((rows, dim), F32),
                   jax.ShapeDtypeStruct(kc.shape, kc.dtype), jax.ShapeDtypeStruct(vc.shape, vc.dtype)],
        in_specs=specs,
        out_specs=[vspec(), vspec(), aspec(), aspec()],
        scratch_shapes=scratch,
        input_output_aliases=alias,
        compiler_params=pltpu.CompilerParams(vmem_limit_bytes=VMEM_LIMIT),
        name=f"layer{layer}",
    )(*ins)


TV = 1024
EBUF = 8


def scores_kernel(nblk, ar_ref, prev_ref, ln_ref, nf_ref, tgt_ref, e_hbm, out_ref, f_ref, ebuf, za, zb, m_ref, s_ref, t_ref, sem):
    rows, dim = f_ref.shape

    def fetch(i, slot):
        return pltpu.make_async_copy(e_hbm.at[pl.ds(pl.multiple_of(i * TV, TV), TV), :], ebuf.at[slot], sem.at[slot])

    for i in range(EBUF - 2):
        fetch(i, i).start()
    hid = prev_ref[...] + rms(ar_ref[...], ln_ref[7:8, :])
    f_ref[...] = rms(hid, nf_ref[...]).astype(BF16)
    m_ref[...] = jnp.full_like(m_ref, -jnp.inf)
    s_ref[...] = jnp.zeros_like(s_ref)
    t_ref[...] = jnp.zeros_like(t_ref)

    def dots(slot, z):
        for c in range(TV // 256):
            z[:, c * 256:(c + 1) * 256] = lax.dot_general(f_ref[...], ebuf[slot, c * 256:(c + 1) * 256, :], NT, preferred_element_type=F32)

    def fold(i, z):
        for r in range(rows // 8):
            sl = slice(r * 8, (r + 1) * 8)
            vals = [z[sl, g * 128:(g + 1) * 128] for g in range(TV // 128)]
            top = m_ref[sl, :]
            tops = list(vals)
            while len(tops) > 1:
                tops = [jnp.maximum(tops[n], tops[n + 1]) for n in range(0, len(tops), 2)]
            new = jnp.maximum(top, tops[0])
            m_ref[sl, :] = new
            exps = [jnp.exp(v - new) for v in vals]
            while len(exps) > 1:
                exps = [exps[n] + exps[n + 1] for n in range(0, len(exps), 2)]
            s_ref[sl, :] = s_ref[sl, :] * jnp.exp(top - new) + exps[0]
            want = tgt_ref[sl, :]
            hit = t_ref[sl, :]
            for g, v in enumerate(vals):
                hit = jnp.where(want == i * TV + g * 128, v, hit)
            t_ref[sl, :] = hit

    def prep(i, slot):
        fetch(i, slot).wait()

    def more(i):
        @pl.when(i < nblk)
        def _():
            fetch(i, lax.rem(i, EBUF)).start()

    fetch(0, 0).wait()
    more(EBUF - 2)
    dots(0, za)

    def pair(n, carry):
        a = 2 * n + 1
        b = a + 1
        prep(a, lax.rem(a, EBUF))
        prep(b, lax.rem(b, EBUF))
        more(a + EBUF - 2)
        more(b + EBUF - 2)
        dots(lax.rem(a, EBUF), zb)
        fold(a - 1, za)
        dots(lax.rem(b, EBUF), za)
        fold(a, zb)
        return carry

    lax.fori_loop(0, (nblk - 2) // 2, pair, 0)
    last = nblk - 1
    prep(last, last % EBUF)
    dots(last % EBUF, zb)
    fold(last - 1, za)
    fold(last, zb)

    m = m_ref[...]
    top = jnp.max(m, axis=-1, keepdims=True)
    tot = jnp.sum(s_ref[...] * jnp.exp(m - top), axis=-1, keepdims=True)
    tgt = jnp.sum(t_ref[...], axis=-1, keepdims=True)
    lane = lax.broadcasted_iota(jnp.int32, (rows, 128), 1)
    pack = jnp.where(lane == 0, top, jnp.where(lane == 1, tot, jnp.where(lane == 2, tgt, 0.0)))
    pad = out_ref.shape[1] - rows
    pack = jnp.concatenate([pack, jnp.zeros((pad, 128), F32)], axis=0)
    out_ref[...] = jnp.transpose(pack)[:8, :]


def table_scores(ar, prev, ln, nf, tgt, table):
    rows, dim = ar.shape
    nblk = table.shape[0] // TV
    lanes = -(-rows // 128) * 128
    return pl.pallas_call(
        functools.partial(scores_kernel, nblk),
        out_shape=jax.ShapeDtypeStruct((8, lanes), F32),
        in_specs=[vspec()] * 5 + [aspec()],
        out_specs=vspec(),
        scratch_shapes=[
            pltpu.VMEM((rows, dim), BF16), pltpu.VMEM((EBUF, TV, dim), BF16),
            pltpu.VMEM((rows, TV), F32), pltpu.VMEM((rows, TV), F32),
            pltpu.VMEM((rows, 128), F32), pltpu.VMEM((rows, 128), F32), pltpu.VMEM((rows, 128), F32),
            pltpu.SemaphoreType.DMA((EBUF,)),
        ],
        compiler_params=pltpu.CompilerParams(vmem_limit_bytes=VMEM_LIMIT),
        name="table_scores",
    )(ar, prev, ln, nf, tgt, table)


def combine_kernel(x_ref, out_ref, got, ssem, rsem):
    dp = lax.axis_index("dp")
    tp = lax.axis_index("tp")
    barrier = pltpu.get_barrier_semaphore()
    for d in range(1, 4):
        pl.semaphore_signal(barrier, inc=1, device_id=(dp, lax.rem(tp + d, 4)), device_id_type=MESH)
    pl.semaphore_wait(barrier, 3)
    sends = []
    for d in range(1, 4):
        sends.append(pltpu.make_async_remote_copy(src_ref=x_ref, dst_ref=got.at[d - 1], send_sem=ssem.at[d - 1], recv_sem=rsem.at[d - 1],
                                                  device_id=(dp, lax.rem(tp + d, 4)), device_id_type=MESH))
        sends[-1].start()
    for s in sends:
        s.wait()
    mine = x_ref[...]
    vals = [mine] + [got[d] for d in range(3)]
    ordered = []
    for dev in range(4):
        v = mine
        for d in range(1, 4):
            v = jnp.where(lax.rem(tp + 4 - d, 4) == dev, vals[d], v)
        ordered.append(v)
    top = jnp.maximum(jnp.maximum(ordered[0][0:1], ordered[1][0:1]), jnp.maximum(ordered[2][0:1], ordered[3][0:1]))
    tot = 0.0
    tgt = 0.0
    for v in ordered:
        tot = tot + v[1:2] * jnp.exp(v[0:1] - top)
        tgt = tgt + v[2:3]
    log_z = top + jnp.log(tot)
    lanes = out_ref.shape[1]
    row = lax.broadcasted_iota(jnp.int32, (8, lanes), 0)
    out_ref[...] = jnp.where(row == 0, tgt - log_z, log_z)


def combine(x, cid):
    return pl.pallas_call(
        combine_kernel,
        out_shape=jax.ShapeDtypeStruct(x.shape, F32),
        in_specs=[vspec()],
        out_specs=vspec(),
        scratch_shapes=[pltpu.VMEM((3,) + x.shape, F32), pltpu.SemaphoreType.DMA((3,)), pltpu.SemaphoreType.DMA((3,))],
        compiler_params=pltpu.CompilerParams(collective_id=cid, has_side_effects=True),
        name="combine_tp",
    )(x)


def solution(mesh):
    arg_specs = (P('dp', None), P('dp', None), P('dp'), P('tp', None), P(), P(), P(), P(), P(), P(), P(None, None, 'tp'), P(None, None, 'tp'), P(None, 'tp', None), P(), P(None, 'dp'), P(None, 'dp'))
    result_specs = (P('dp', None), P('dp', None), P(None, 'dp'), P(None, 'dp'))

    def decode_local(tokens, targets, start_pos, embed_table, layer_norms, w_q, w_k, w_v, qk_norms, w_o, w_gate, w_up, w_down, norm_final, k_cache, v_cache):
        batch, steps = tokens.shape
        layers, dim, heads, head_dim = w_q.shape
        window = k_cache.shape[2]
        vocab_local = embed_table.shape[0]
        rows = batch * steps
        vocab_start = lax.axis_index('tp') * vocab_local
        positions = (start_pos[None, :] + jnp.arange(steps)[:, None]).reshape(rows)
        inv_freq = ROPE_BASE ** (-2.0 * jnp.arange(head_dim // 2, dtype=F32) / head_dim)
        angles = positions.astype(F32)[:, None] * inv_freq[None, :]
        startv = jnp.broadcast_to(start_pos[:, None, None], (batch, 16, 128)).reshape(batch * 16, 128)
        ln = layer_norms.reshape(layers * 4, dim)
        small = (start_pos, startv, jnp.cos(angles), jnp.sin(angles), ln, qk_norms.reshape(layers * 2, head_dim))
        weights = (w_q.reshape(layers, dim, heads * head_dim), w_k.reshape(layers, dim, head_dim), w_v.reshape(layers, dim, head_dim),
                   w_o.reshape(layers, heads * head_dim, dim), jnp.swapaxes(w_gate, 1, 2), jnp.swapaxes(w_up, 1, 2), w_down)
        caches = (k_cache.reshape(layers, batch, window, head_dim), v_cache.reshape(layers, batch, window, head_dim))
        ar = sum_tp(gather_rows(tokens.T.reshape(rows) - vocab_start, embed_table), 0)
        hid, outs = None, None
        for layer in range(layers):
            hid, part, kc, vc = run_layer(layer, small, ar, hid, weights, caches, outs)
            outs = (kc, vc)
            ar = sum_tp(part, 1 + layer)
        tgt = (targets.T.reshape(rows) - vocab_start)[:, None] - jnp.arange(128)[None, :]
        stats = table_scores(ar, hid, ln, norm_final.reshape(1, dim), tgt, embed_table)
        res = combine(stats, 1 + layers)
        logprob = res[0, :rows].reshape(steps, batch).T
        log_z = res[1, :rows].reshape(steps, batch).T
        return logprob, log_z, outs[0].reshape(k_cache.shape), outs[1].reshape(v_cache.shape)

    return jax.shard_map(decode_local, mesh=mesh, in_specs=arg_specs, out_specs=result_specs, check_vma=False)
```

time: 1170 us -> 261 us (0.22); the launches traced: 1160 us -> 261 us
  matrix products: 418 us -> 0 us
  local copies, waits for them, and re-layouts: 380 us -> 20.6 us
  waiting for transfers between devices: 247 us -> 0 us
  Pallas kernels: 0 us -> 235 us
  other arithmetic: 84.1 us -> 4.18 us
  between operations: 15.9 us -> 0.79 us
    dot_general x51 -> x0, matrix products: 418 us -> none  [the longest x3 198 us: decode_local(): jnp.einsum('bd,vd->bv', final_normed, embed_table, preferred_element_type...]
    psum x9 -> x0, waiting for transfers between devices: 247 us -> none  [the longest x4 122 us: decode_local(): lax.psum(down_part, 'tp')]
    pallas_call x0 -> x8, Pallas kernels: none -> 235 us  [the longest x2 92.9 us: run_layer(): pl.pallas_call(functools.partial(layer_kernel, layer, batch, steps, norma...]
    unnamed x116 -> x20, local copies, waits for them, and re-layouts: 202 us -> 6.01 us
    scatter x12 -> x0, local copies, waits for them, and re-layouts: 137 us -> none  [the longest x6 68.4 us: decode_local(): k_cache = k_cache.at[layer_idx, row_ids, slot_now].set(keys_new)]
    reduce_sum x32 -> x0, other arithmetic: 61.2 us -> none  [the longest x3 31 us: decode_local(): exp_sum = jnp.sum(jnp.exp(logits - top_logit[:, None]), axis=-1)]
    gather x6 -> x0, local copies, waits for them, and re-layouts: 27 us -> none  [the longest x3 17.3 us: decode_local(): jnp.take(embed_table, jnp.clip(tok_local, 0, vocab_local - 1), axis=0)]
  transfers between devices with their start and end apart: 9 -> 0, of which waited for: 9 -> 0; matrix products, arithmetic and copies ran while one was open for 3% -> 0% of each run, Pallas kernels for 0% -> 0%
where the time goes in v1:
time: 261 us
  Pallas kernels  235 us (90%)
  local copies, waits for them, and re-layouts  20.6 us (8%)
  other arithmetic  4.18 us (2%)
    pallas_call x2, Pallas kernels, run_layer(): pl.pallas_call(functools.partial(layer_kernel, layer, batch, steps, norma...  92.9 us
    pallas_call x1, Pallas kernels, table_scores(): pl.pallas_call(functools.partial(scores_kernel, nblk), out_shape=jax.Shap...  65.2 us
    pallas_call x3, Pallas kernels, sum_tp(): pl.pallas_call(functools.partial(sum_kernel, rows, chunks), out_shape=jax...  61.7 us
    pallas_call x1, Pallas kernels, gather_rows(): pl.pallas_call(functools.partial(gather_kernel, rows), out_shape=jax.Shap...  10.2 us
    reshape x1, local copies, waits for them, and re-layouts, decode_local(): w_q.reshape(layers, dim, heads * head_dim)  8.72 us
    unnamed x20, local copies, waits for them, and re-layouts  6.01 us

profile of v1, /device:TPU:0, one launch (start us, length us, event | category | flops | bytes accessed | tf_op | source)
XLA Modules:
  0.0 260.8 jit_solution(529547952739245249)
XLA Ops:
  0.6 1.3 subtract_bitcast_fusion
  1.9 0.2 min.19
  2.1 0.7 and_bitcast_fusion
  2.8 0.2 and.63
  3.0 0.1 fusion.2.col_ref
  3.1 0.1 min.17
  3.2 0.0 copy-start.8
  3.2 0.0 copy-start.5
  3.2 10.2 %token_rows.1.part_ref = f32[288,1152]{1,0:T(8,128)S(1)} custom-call(s32[288]{0:T(512)S(1)} %add_select_fusion.2.grp_ref, s32[288,1]{1,0:T(8,128)S(1)} %fusion.2.col_ref, bf16[65536,1152]{1,0:T(8,128)(2,1)} %e_hbm.1), custom_call_target="tpu_custom_call" | custom-call | tf_op jit(solution)/shard_map/token_rows/pallas_call | solution.py:59
  13.4 21.7 %sum_tp.3.refs_6_ = f32[288,1152]{1,0:T(8,128)S(1)} custom-call(f32[288,1152]{1,0:T(8,128)S(1)} %token_rows.1.part_ref), custom_call_target="tpu_custom_call" | custom-call | tf_op jit(solution)/shard_map/sum_tp/pallas_call | solution.py:122
  35.1 0.0 copy-start
  35.1 1.1 copy-done
  36.2 0.0 copy-done.8
  36.2 0.1 convert_element_type.11
  36.3 1.3 multiply_sine_fusion
  37.6 0.0 copy-done.5
  37.6 0.6 reshape.175.refs_4_.ln_ref
  38.3 0.0 copy-start.9
  38.3 8.7 %reshape.177.refs_7_.refs_8_ = bf16[2,1152,1024]{2,1,0:T(8,128)(2,1)} reshape(bf16[2,1152,4,256]{3,2,1,0:T(4,128)(2,1)} %param.21) | data formatting | bytes 9437184 | tf_op jit(solution)/shard_map/reshape | solution.py:518
  47.0 0.1 broadcast_in_dim.10
  47.1 0.1 broadcast_in_dim.11
  47.1 1.2 broadcast_in_dim.12.refs_1_
  48.3 0.0 copy-done.9
  48.3 0.6 reshape.176.refs_5_
  49.0 46.2 %layer0.1 = (f32[288,1152]{1,0:T(8,128)}, f32[288,1152]{1,0:T(8,128)}, bf16[2,96,512,256]{3,2,1,0:T(8,128)(2,1)}, bf16[2,96,512,256]{3,2,1,0:T(8,128)(2,1)}) custom-call(s32[96]{0:T(128)} %refs_0_.3, s32[1536,128]{1,0:T(8,128)} %broadcast_in_dim.12.refs_1_, f32[288,128]{1,0:T(8,128)} %get-tuple-element.31.refs_2_, f32[288,128]{1,0:T(8,128)} %get-tuple-element.30.refs_3_, ...), custom_call_target="tpu_custom_call" | custom-call | tf_op jit(solution)/shard_map/layer0/pallas_call | solution.py:337
  95.2 0.0 copy-start.4
  95.2 1.3 copy-done.4
  96.5 20.2 %sum_tp.4.refs_6_ = f32[288,1152]{1,0:T(8,128)S(1)} custom-call(f32[288,1152]{1,0:T(8,128)S(1)} %copy-done.4), custom_call_target="tpu_custom_call" | custom-call | tf_op jit(solution)/shard_map/sum_tp/pallas_call | solution.py:122
  116.7 0.0 copy-start.2
  116.7 1.2 copy-done.2
  117.9 0.0 copy-start.6
  117.9 0.0 copy-start.7
  117.9 46.7 %layer1.1 = (f32[288,1152]{1,0:T(8,128)}, f32[288,1152]{1,0:T(8,128)}, bf16[2,96,512,256]{3,2,1,0:T(8,128)(2,1)}, bf16[2,96,512,256]{3,2,1,0:T(8,128)(2,1)}) custom-call(s32[96]{0:T(128)} %refs_0_.3, s32[1536,128]{1,0:T(8,128)} %broadcast_in_dim.12.refs_1_, f32[288,128]{1,0:T(8,128)} %get-tuple-element.31.refs_2_, ...), custom_call_target="tpu_custom_call", output_to_operand_aliasing={{2}: (17, {}), {3}: (18, {})} | custom-call | tf_op jit(solution)/shard_map/layer1/pallas_call | solution.py:337
  164.6 0.0 copy-start.3
  164.6 1.3 copy-done.3
  165.9 19.9 %sum_tp.5.ar_ref = f32[288,1152]{1,0:T(8,128)S(1)} custom-call(f32[288,1152]{1,0:T(8,128)S(1)} %copy-done.3), custom_call_target="tpu_custom_call" | custom-call | tf_op jit(solution)/shard_map/sum_tp/pallas_call | solution.py:122
  185.8 0.0 copy-start.1
  185.8 1.1 copy-done.1
  186.9 0.0 copy-done.6
  186.9 0.1 sub.55
  187.0 0.8 iota_subtract_fusion.tgt_ref
  187.8 0.0 copy-done.7
  187.8 0.6 reshape.183.nf_ref
  188.4 65.2 %table_scores.1.x_ref = f32[8,384]{1,0:T(8,128)} custom-call(f32[288,1152]{1,0:T(8,128)} %copy-done.1, f32[288,1152]{1,0:T(8,128)} %get-tuple-element.17.prev_ref, f32[8,1152]{1,0:T(8,128)} %reshape.175.refs_4_.ln_ref, f32[1,1152]{1,0:T(1,128)} %reshape.183.nf_ref, s32[288,128]{1,0:T(8,128)} %iota_subtract_fusion.tgt_ref, bf16[65536,1152]{1,0:T(8,128)(2,1)} %e_hbm.1), custom_call_target="tpu_custom_call" | custom-call | tf_op jit(solution)/shard_map/table_scores/pallas_call | solution.py:439
  253.6 5.1 %combine_tp.1 = f32[8,384]{1,0:T(8,128)} custom-call(f32[8,384]{1,0:T(8,128)} %table_scores.1.x_ref), custom_call_target="tpu_custom_call" | custom-call | tf_op jit(solution)/shard_map/combine_tp/pallas_call | solution.py:490
  258.7 0.8 slice_reduce_fusion
  259.5 0.7 reshape_squeeze.6
  260.1 0.7 reshape_squeeze.7
  (3 shorter events, 0.0 us)
Async XLA Ops:
  3.2 33.0 %copy-start.8 = (s32[96]{0:T(128)S(1)}, s32[96]{0:T(128)}, u32[]{:S(2)}) copy-start(s32[96]{0:T(128)} %refs_0_.3) | copy-start | bytes 1156
  3.2 34.5 %copy-start.5 = (f32[2,4,1152]{2,1,0:T(4,128)S(1)}, f32[2,4,1152]{2,1,0:T(4,128)}, u32[]{:S(2)}) copy-start(f32[2,4,1152]{2,1,0:T(4,128)} %param.20) | copy-start | bytes 110596
  35.1 1.1 copy-start
  38.3 10.1 %copy-start.9 = (f32[2,2,256]{2,1,0:T(2,128)S(1)}, f32[2,2,256]{2,1,0:T(2,128)}, u32[]{:S(2)}) copy-start(f32[2,2,256]{2,1,0:T(2,128)} %param.24) | copy-start | bytes 12292
  95.2 1.3 copy-start.4
  116.7 1.2 copy-start.2
  117.9 69.0 %copy-start.6 = (s32[3,96]{1,0:T(4,128)S(1)}, s32[3,96]{1,0:T(4,128)}, u32[]{:S(2)}) copy-start(s32[3,96]{1,0:T(4,128)} %get-tuple-element.32) | copy-start | bytes 3460
  117.9 69.9 %copy-start.7 = (f32[1152]{0:T(1024)S(1)}, f32[1152]{0:T(1024)}, u32[]{:S(2)}) copy-start(f32[1152]{0:T(1024)} %param.29) | copy-start | bytes 13828
  164.6 1.3 copy-start.3
  185.8 1.1 copy-start.1

commit v2 on v1

v2 whole, which is shorter than its diff:
```python
import functools

import jax
import jax.numpy as jnp
import numpy as np
from jax import lax
from jax.experimental import pallas as pl
from jax.experimental.pallas import tpu as pltpu
from jax.sharding import PartitionSpec as P

EPSILON = 1e-6
ROPE_BASE = 10000.0
NEG = -1e30
MESH = pl.DeviceIdType.MESH
F32 = jnp.float32
BF16 = jnp.bfloat16
NT = (((1,), (1,)), ((), ()))


def rms(values, weight):
    mean_sq = jnp.mean(values * values, axis=-1, keepdims=True)
    return values * lax.rsqrt(mean_sq + EPSILON) * (1.0 + weight)


def vspec():
    return pl.BlockSpec(memory_space=pltpu.VMEM)


def aspec():
    return pl.BlockSpec(memory_space=pl.ANY)


def sspec():
    return pl.BlockSpec(memory_space=pltpu.SMEM)


def gather_kernel(rows, grp_ref, col_ref, table_ref, out_ref, xbuf, sem):
    def issue(i, carry):
        src = pl.multiple_of(grp_ref[i] * 8, 8)
        dst = pl.multiple_of(i * 8, 8)
        pltpu.make_async_copy(table_ref.at[pl.ds(src, 8), :], xbuf.at[pl.ds(dst, 8), :], sem).start()
        return carry

    lax.fori_loop(0, rows, issue, 0, unroll=8)
    pltpu.make_async_copy(table_ref.at[pl.ds(0, rows * 8), :], xbuf, sem).wait()
    for c in range(rows // 32):
        lanes = lax.broadcasted_iota(jnp.int32, (32, 256), 1)
        pick = jnp.where(lanes == col_ref[c * 32:(c + 1) * 32, :], 1.0, 0.0).astype(BF16)
        out_ref[c * 32:(c + 1) * 32, :] = jnp.dot(pick, xbuf[c * 256:(c + 1) * 256, :], preferred_element_type=F32)


def gather_rows(ids, table):
    rows = ids.shape[0]
    vocab_local, dim = table.shape
    here = (ids >= 0) & (ids < vocab_local)
    safe = jnp.clip(ids, 0, vocab_local - 1)
    col = jnp.where(here, (jnp.arange(rows) % 32) * 8 + safe % 8, -1)[:, None]
    return pl.pallas_call(
        functools.partial(gather_kernel, rows),
        out_shape=jax.ShapeDtypeStruct((rows, dim), F32),
        in_specs=[sspec(), vspec(), aspec()],
        out_specs=vspec(),
        scratch_shapes=[pltpu.VMEM((rows * 8, dim), BF16), pltpu.SemaphoreType.DMA],
        compiler_params=pltpu.CompilerParams(vmem_limit_bytes=24 * 1024 * 1024),
        name="token_rows",
    )(safe // 8, col, table)


LANES = 128
HEAD = 2 * LANES
TILE = 16
WINDOW = 512
MIB = 1024 * 1024


def mate_of():
    tp = lax.axis_index("tp")
    core = lax.rem(tp, 2)
    return core, (lax.axis_index("dp"), tp + 1 - 2 * core)


def meet(mate):
    barrier = pltpu.get_barrier_semaphore()
    pl.semaphore_signal(barrier, inc=1, device_id=mate, device_id_type=MESH)
    pl.semaphore_wait(barrier, 1)


def send(src, dst, ssem, rsem, peer):
    return pltpu.make_async_remote_copy(src_ref=src, dst_ref=dst, send_sem=ssem, recv_sem=rsem, device_id=peer, device_id_type=MESH)


def part_rows(which, ref):
    hrows = ref.shape[0] // 2
    return pl.ds(pl.multiple_of(which * hrows, 8), hrows)


def mate_sum(part_ref, out_ref, got, ssem, rsem, core, mate):
    swap = send(part_ref.at[part_rows(1 - core, part_ref), :], got, ssem, rsem, mate)
    swap.start()
    swap.wait()
    out_ref[...] = part_ref[part_rows(core, part_ref), :] + got[...]


def pair_sum_kernel(part_ref, out_ref, got, ssem, rsem):
    core, mate = mate_of()
    meet(mate)
    mate_sum(part_ref, out_ref, got, ssem, rsem, core, mate)


def pair_share_kernel(a_ref, b_ref, out_ref, total, got, ssem, rsem):
    core, mate = mate_of()
    total[...] = a_ref[...] + b_ref[...]
    meet(mate)
    swap = send(total, got, ssem, rsem, mate)
    swap.start()
    out_ref[part_rows(core, out_ref), :] = total[...]
    swap.wait()
    out_ref[part_rows(1 - core, out_ref), :] = got[...]


def pair_call(kernel, out_rows, ins, scratch, cid, name):
    dim = ins[0].shape[1]
    return pl.pallas_call(
        kernel,
        out_shape=jax.ShapeDtypeStruct((out_rows, dim), F32),
        in_specs=[vspec()] * len(ins),
        out_specs=vspec(),
        scratch_shapes=[pltpu.VMEM(shape, F32) for shape in scratch] + [pltpu.SemaphoreType.DMA] * 2,
        compiler_params=pltpu.CompilerParams(collective_id=cid, has_side_effects=True, vmem_limit_bytes=12 * MIB),
        name=name,
    )(*ins)


def pair_sum(part, cid):
    rows, dim = part.shape
    return pair_call(pair_sum_kernel, rows // 2, [part], [(rows // 2, dim)], cid, "pair_sum")


def share(half, cid):
    far = lax.ppermute(half, 'tp', [(n, (n + 2) % 4) for n in range(4)])
    return pair_call(pair_share_kernel, half.shape[0] * 2, [half, far], [half.shape] * 2, cid, "pair_share")


NB = 8
NBUF = 4


class Stream:
    def __init__(self, layer, base, sources, targets, bufs, rsem, osem):
        self.layer, self.base = layer, base
        self.sources, self.targets, self.bufs, self.rsem, self.osem = sources, targets, bufs, rsem, osem

    def rows(self, i):
        return pl.ds(pl.multiple_of(self.base + i * NB, NB), NB)

    def reads(self, i, slot):
        return [pltpu.make_async_copy(src.at[self.layer, self.rows(i)], buf.at[slot], self.rsem.at[n, slot])
                for n, (src, buf) in enumerate(zip(self.sources, self.bufs))]

    def writes(self, i, slot):
        return [pltpu.make_async_copy(buf.at[slot], dst.at[self.layer, self.rows(i)], self.osem.at[n, slot])
                for n, (dst, buf) in enumerate(zip(self.targets, self.bufs))]

    def begin(self):
        for i in range(2):
            for c in self.reads(i, i):
                c.start()

    def run(self, nblk, body):
        def block(i, carry):
            slot = lax.rem(i, NBUF)
            for c in self.reads(i, slot):
                c.wait()

            @pl.when(i >= 1)
            def _():
                for c in self.writes(i - 1, lax.rem(i + NBUF - 1, NBUF)):
                    c.start()

            @pl.when(i >= 2)
            def _():
                for c in self.writes(i - 2, lax.rem(i + NBUF - 2, NBUF)):
                    c.wait()

            @pl.when(i + 2 < nblk)
            def _():
                for c in self.reads(i + 2, lax.rem(i + 2, NBUF)):
                    c.start()

            body(i, slot)
            return carry

        lax.fori_loop(0, nblk, block, 0)
        for c in self.writes(nblk - 1, (nblk - 1) % NBUF):
            c.start()

    def end(self, nblk):
        for i in (nblk - 2, nblk - 1):
            for c in self.writes(i, i % NBUF):
                c.wait()

    def change(self, i, slot, start_ref, fresh, steps):
        sub = lax.broadcasted_iota(jnp.int32, (TILE, HEAD), 0)
        for first in (0, NB // 2):
            pending = []
            for j in range(first, first + NB // 2):
                st = start_ref[self.base + i * NB + j]
                for s in (st & (WINDOW - 1), (st + steps - 1) & (WINDOW - 1)):
                    at = pl.multiple_of(s - (s & (TILE - 1)), TILE)
                    dist = (sub + at - st) & (WINDOW - 1)
                    for buf, new in zip(self.bufs, fresh):
                        value = buf[slot, j, pl.ds(at, TILE), :].astype(F32)
                        for t in range(steps):
                            value = jnp.where(dist == t, new[TILE * j + t:TILE * j + t + 1, :], value)
                        pending.append((buf, j, at, value.astype(BF16)))
            for buf, j, at, value in pending:
                buf[slot, j, pl.ds(at, TILE), :] = value


def stream_scratch():
    buf = pltpu.VMEM((NBUF, NB, WINDOW, HEAD), BF16)
    sem = pltpu.SemaphoreType.DMA((2, NBUF))
    return [buf, buf, sem, sem]


def cache_shapes(caches):
    return [jax.ShapeDtypeStruct(c.shape, c.dtype) for c in caches]


def wide(ref, n, at):
    return jnp.concatenate([ref[n, at, :], ref[n + 1, at, :]], axis=1)


def tiles(i):
    return pl.ds(pl.multiple_of(i * NB * TILE, NB * TILE), NB * TILE)


def carry_kernel(layer, steps, core_ref, start_ref, fresh, k_hbm, v_hbm, _k, _v, ko_hbm, vo_hbm, kbuf, vbuf, rsem, osem):
    half = fresh.shape[1] // TILE
    nblk = half // NB
    stream = Stream(layer, (1 - core_ref[0]) * half, (k_hbm, v_hbm), (ko_hbm, vo_hbm), (kbuf, vbuf), rsem, osem)
    stream.begin()
    stream.run(nblk, lambda i, slot: stream.change(i, slot, start_ref, (wide(fresh, 0, tiles(i)), wide(fresh, 2, tiles(i))), steps))
    stream.end(nblk)


def carry_other(layer, steps, core, start, fresh, caches, outs):
    return pl.pallas_call(
        functools.partial(carry_kernel, layer, steps),
        out_shape=cache_shapes(caches),
        in_specs=[sspec(), sspec(), vspec()] + [aspec()] * 4,
        out_specs=[aspec()] * 2,
        scratch_shapes=stream_scratch(),
        input_output_aliases={5: 0, 6: 1},
        compiler_params=pltpu.CompilerParams(vmem_limit_bytes=24 * MIB),
        cost_estimate=pl.CostEstimate(flops=10 ** 10, bytes_accessed=48 * MIB, transcendentals=0),
        name=f"carry{layer}",
    )(core, start, fresh, *caches, *outs)


def feed_kernel(layer, heads_ref, hid_ref, ln_ref, wo_hbm, wg_hbm, wu_hbm, wd_hbm,
                hid_out, half_ref, wo, wg, wu, wd, both, part, got, wsem, hsend, hrecv, ssem, rsem):
    core, mate = mate_of()
    weights = [(wo_hbm, wo), (wg_hbm, wg), (wu_hbm, wu), (wd_hbm, wd)]
    wcopies = [pltpu.make_async_copy(src.at[layer], dst, wsem.at[n]) for n, (src, dst) in enumerate(weights)]
    for c in wcopies:
        c.start()
    meet(mate)
    swap = send(heads_ref, both.at[core], hsend, hrecv, mate)
    swap.start()
    both[core] = heads_ref[...]
    ln = lambda j: ln_ref[4 * layer + j:4 * layer + j + 1, :]
    wcopies[0].wait()
    swap.wait_recv()
    x = jnp.concatenate([both[0], both[1]], axis=0).astype(BF16)
    hid = hid_ref[...] + rms(jnp.dot(x, wo[...], preferred_element_type=F32), ln(1))
    hid_out[...] = hid
    act = rms(hid, ln(2)).astype(BF16)
    for c in wcopies[1:]:
        c.wait()
    width = wg.shape[0]
    for at in range(0, width, WINDOW):
        cut = slice(at, min(at + WINDOW, width))
        gate = lax.dot_general(act, wg[cut, :], NT, preferred_element_type=F32)
        up = lax.dot_general(act, wu[cut, :], NT, preferred_element_type=F32)
        inner = (jax.nn.gelu(gate, approximate=True) * up).astype(BF16)
        down = jnp.dot(inner, wd[cut, :], preferred_element_type=F32)
        if at == 0:
            part[...] = down
        else:
            part[...] += down
    swap.wait_send()
    mate_sum(part, half_ref, got, ssem, rsem, core, mate)


def feed(layer, heads, hid, ln, weights, cid):
    rows, dim = hid.shape
    width = weights[1].shape[1]
    own, inner = heads.shape
    return pl.pallas_call(
        functools.partial(feed_kernel, layer),
        out_shape=[jax.ShapeDtypeStruct((rows, dim), F32), jax.ShapeDtypeStruct((own, dim), F32)],
        in_specs=[vspec()] * 3 + [aspec()] * 4,
        out_specs=[vspec()] * 2,
        scratch_shapes=[pltpu.VMEM((inner, dim), BF16)] + [pltpu.VMEM((width, dim), BF16)] * 3 + [
            pltpu.VMEM((2, own, inner), F32), pltpu.VMEM((rows, dim), F32), pltpu.VMEM((own, dim), F32),
            pltpu.SemaphoreType.DMA((4,))] + [pltpu.SemaphoreType.DMA] * 4,
        compiler_params=pltpu.CompilerParams(collective_id=cid, has_side_effects=True, vmem_limit_bytes=40 * MIB),
        name=f"feed{layer}",
    )(heads, hid, ln, *weights)


def attend_kernel(layer, steps, normalizer, *refs):
    core_ref, start_ref, startv_ref, cos_ref, sin_ref, ln_ref, qk_ref, ar_ref, *refs = refs
    if layer == 0:
        wq_hbm, wk_hbm, wv_hbm, k_hbm, v_hbm, *refs = refs
    else:
        prev_ref, wq_hbm, wk_hbm, wv_hbm, k_hbm, v_hbm, _, _, *refs = refs
    hid_ref, heads_ref, fresh_hbm, ko_hbm, vo_hbm, wq, wk, wv, qs, fresh, os, wsem, fsem, kbuf, vbuf, rsem, osem = refs
    heads = wq.shape[1] // HEAD
    half = qs.shape[1] // TILE
    nblk = half // NB
    hrows = half * steps
    core = core_ref[0]
    ln = lambda l, j: ln_ref[4 * l + j:4 * l + j + 1, :]
    weights = [(wq_hbm, wq), (wk_hbm, wk), (wv_hbm, wv)]
    wcopies = [pltpu.make_async_copy(src.at[layer], dst, wsem.at[n]) for n, (src, dst) in enumerate(weights)]
    stream = Stream(layer, core * half, (k_hbm, v_hbm), (ko_hbm, vo_hbm), (kbuf, vbuf), rsem, osem)
    for c in wcopies:
        c.start()
    stream.begin()

    if layer == 0:
        hid = ar_ref[...] * normalizer
    else:
        hid = prev_ref[...] + rms(ar_ref[...], ln(layer - 1, 3))
    hid_ref[...] = hid
    qs[...] = jnp.zeros_like(qs)
    fresh[...] = jnp.zeros_like(fresh)
    act = rms(hid, ln(layer, 0)).astype(BF16)
    for c in wcopies:
        c.wait()

    def roped(x, weight, at):
        x = rms(x, weight)
        a, b = x[:, :LANES], x[:, LANES:]
        c, s = cos_ref[at, :], sin_ref[at, :]
        return a * c - b * s, b * c + a * s

    def put_fresh(kv, pair):
        for c in range(2):
            for t in range(steps):
                r = c * hrows + t * half
                for g in range(2):
                    fresh[2 * kv + g, pl.ds(c * half * TILE + t, half, stride=TILE), :] = pair[g][r:r + half, :]

    k = jnp.dot(act, wk[...], preferred_element_type=F32)
    put_fresh(0, roped(k, qk_ref[2 * layer + 1:2 * layer + 2, :], slice(None)))
    v = jnp.dot(act, wv[...], preferred_element_type=F32)
    put_fresh(1, (v[:, :LANES], v[:, LANES:]))
    away = pl.ds(pl.multiple_of((1 - core) * half * TILE, TILE), half * TILE)
    keep = pltpu.make_async_copy(fresh.at[:, away, :], fresh_hbm, fsem)

    mine = pl.ds(pl.multiple_of(core * hrows, 8), hrows)
    own = rms(hid_ref[mine, :], ln(layer, 0)).astype(BF16)
    for h in range(heads):
        q = jnp.dot(own, wq[:, h * HEAD:(h + 1) * HEAD], preferred_element_type=F32)
        pair = roped(q, qk_ref[2 * layer:2 * layer + 1, :], mine)
        for g in range(2):
            for t in range(steps):
                qs[g, pl.ds(t * heads + h, half, stride=TILE), :] = pair[g][t * half:(t + 1) * half, :]

    scale = HEAD ** -0.5
    m_rows = NB * TILE

    def body(i, slot):
        at = tiles(i)
        gat = tiles(core * nblk + i)
        qb = wide(qs, 0, at).astype(BF16)
        kf = wide(fresh, 0, gat)
        vf = wide(fresh, 2, gat)
        start = startv_ref[gat, :]
        row = lax.broadcasted_iota(jnp.int32, (m_rows, LANES), 0)
        lane = lax.broadcasted_iota(jnp.int32, (m_rows, LANES), 1)
        t = lax.shift_right_logical(row & (TILE - 1), 2)
        old = jnp.concatenate([lax.dot_general(qb[TILE * j:TILE * (j + 1), :], kbuf[slot, j], NT, preferred_element_type=F32) for j in range(NB)], axis=0) * scale
        new = lax.dot_general(qb, kf.astype(BF16), NT, preferred_element_type=F32) * scale
        cols = []
        for g in range(0, WINDOW, LANES):
            s = lane + g
            ok = (s <= start + t) & (((s - start) & (WINDOW - 1)) > t)
            cols.append(jnp.where(ok, old[:, g:g + LANES], NEG))
        ok = (row - (row & (TILE - 1)) == lane - (lane & (TILE - 1))) & ((lane & (TILE - 1)) <= t)
        cols.append(jnp.where(ok, new, NEG))
        top = functools.reduce(jnp.maximum, cols)
        top = jnp.max(top, axis=-1, keepdims=True)
        exps = [jnp.exp(c - top) for c in cols]
        tot = jnp.sum(functools.reduce(jnp.add, exps), axis=-1, keepdims=True)
        inv = 1.0 / tot
        pold = jnp.concatenate([(e * inv).astype(BF16) for e in exps[:-1]], axis=1)
        pnew = (exps[-1] * inv).astype(BF16)
        out = jnp.dot(pnew, vf.astype(BF16), preferred_element_type=F32)
        out = out + jnp.concatenate([jnp.dot(pold[TILE * j:TILE * (j + 1), :], vbuf[slot, j], preferred_element_type=F32) for j in range(NB)], axis=0)
        os[0, at, :] = out[:, :LANES]
        os[1, at, :] = out[:, LANES:]
        stream.change(i, slot, start_ref, (kf, vf), steps)

    keep.start()
    stream.run(nblk, body)
    for h in range(heads):
        for g in range(2):
            for t in range(steps):
                value = os[g, pl.ds(t * heads + h, half, stride=TILE), :].astype(BF16).astype(F32)
                col = h * HEAD + g * LANES
                heads_ref[t * half:(t + 1) * half, col:col + LANES] = value
    keep.wait()
    stream.end(nblk)


def attend(layer, small, ar, prev, weights, caches, outs):
    batch = caches[0].shape[1]
    rows, dim = ar.shape
    half = batch // 2
    inner = weights[0].shape[2]
    normalizer = float(np.float32(dim ** 0.5).astype(BF16))
    ins = list(small) + [ar] + ([] if prev is None else [prev]) + list(weights) + list(caches)
    specs = [sspec()] * 2 + [vspec()] * (len(ins) - 7) + [aspec()] * 5
    alias = {}
    if outs is not None:
        alias = {len(ins): 3, len(ins) + 1: 4}
        ins += list(outs)
        specs += [aspec()] * 2
    return pl.pallas_call(
        functools.partial(attend_kernel, layer, rows // batch, normalizer),
        out_shape=[jax.ShapeDtypeStruct((rows, dim), F32), jax.ShapeDtypeStruct((rows // 2, inner), F32),
                   jax.ShapeDtypeStruct((4, half * TILE, LANES), F32)] + cache_shapes(caches),
        in_specs=specs,
        out_specs=[vspec(), vspec()] + [aspec()] * 3,
        scratch_shapes=[
            pltpu.VMEM((dim, inner), BF16), pltpu.VMEM((dim, HEAD), BF16), pltpu.VMEM((dim, HEAD), BF16),
            pltpu.VMEM((2, half * TILE, LANES), F32), pltpu.VMEM((4, batch * TILE, LANES), F32), pltpu.VMEM((2, half * TILE, LANES), F32),
            pltpu.SemaphoreType.DMA((3,)), pltpu.SemaphoreType.DMA,
        ] + stream_scratch(),
        input_output_aliases=alias,
        compiler_params=pltpu.CompilerParams(vmem_limit_bytes=42 * MIB),
        name=f"attend{layer}",
    )(*ins)


TV = 1024
EBUF = 8


def scores_kernel(nblk, ar_ref, prev_ref, ln_ref, nf_ref, tgt_ref, e_hbm, out_ref, f_ref, ebuf, za, zb, m_ref, s_ref, t_ref, sem):
    rows, dim = f_ref.shape

    def fetch(i, slot):
        return pltpu.make_async_copy(e_hbm.at[pl.ds(pl.multiple_of(i * TV, TV), TV), :], ebuf.at[slot], sem.at[slot])

    for i in range(EBUF - 2):
        fetch(i, i).start()
    hid = prev_ref[...] + rms(ar_ref[...], ln_ref[7:8, :])
    f_ref[...] = rms(hid, nf_ref[...]).astype(BF16)
    m_ref[...] = jnp.full_like(m_ref, -jnp.inf)
    s_ref[...] = jnp.zeros_like(s_ref)
    t_ref[...] = jnp.zeros_like(t_ref)

    def dots(slot, z):
        for c in range(TV // 256):
            z[:, c * 256:(c + 1) * 256] = lax.dot_general(f_ref[...], ebuf[slot, c * 256:(c + 1) * 256, :], NT, preferred_element_type=F32)

    def fold(i, z):
        for r in range(rows // 8):
            sl = slice(r * 8, (r + 1) * 8)
            vals = [z[sl, g * 128:(g + 1) * 128] for g in range(TV // 128)]
            top = m_ref[sl, :]
            tops = list(vals)
            while len(tops) > 1:
                tops = [jnp.maximum(tops[n], tops[n + 1]) for n in range(0, len(tops), 2)]
            new = jnp.maximum(top, tops[0])
            m_ref[sl, :] = new
            exps = [jnp.exp(v - new) for v in vals]
            while len(exps) > 1:
                exps = [exps[n] + exps[n + 1] for n in range(0, len(exps), 2)]
            s_ref[sl, :] = s_ref[sl, :] * jnp.exp(top - new) + exps[0]
            want = tgt_ref[sl, :]
            hit = t_ref[sl, :]
            for g, v in enumerate(vals):
                hit = jnp.where(want == i * TV + g * 128, v, hit)
            t_ref[sl, :] = hit

    def prep(i, slot):
        fetch(i, slot).wait()

    def more(i):
        @pl.when(i < nblk)
        def _():
            fetch(i, lax.rem(i, EBUF)).start()

    fetch(0, 0).wait()
    more(EBUF - 2)
    dots(0, za)

    def pair(n, carry):
        a = 2 * n + 1
        b = a + 1
        prep(a, lax.rem(a, EBUF))
        prep(b, lax.rem(b, EBUF))
        more(a + EBUF - 2)
        more(b + EBUF - 2)
        dots(lax.rem(a, EBUF), zb)
        fold(a - 1, za)
        dots(lax.rem(b, EBUF), za)
        fold(a, zb)
        return carry

    lax.fori_loop(0, (nblk - 2) // 2, pair, 0)
    last = nblk - 1
    prep(last, last % EBUF)
    dots(last % EBUF, zb)
    fold(last - 1, za)
    fold(last, zb)

    m = m_ref[...]
    top = jnp.max(m, axis=-1, keepdims=True)
    tot = jnp.sum(s_ref[...] * jnp.exp(m - top), axis=-1, keepdims=True)
    tgt = jnp.sum(t_ref[...], axis=-1, keepdims=True)
    lane = lax.broadcasted_iota(jnp.int32, (rows, 128), 1)
    pack = jnp.where(lane == 0, top, jnp.where(lane == 1, tot, jnp.where(lane == 2, tgt, 0.0)))
    pad = out_ref.shape[1] - rows
    pack = jnp.concatenate([pack, jnp.zeros((pad, 128), F32)], axis=0)
    out_ref[...] = jnp.transpose(pack)[:8, :]


def table_scores(ar, prev, ln, nf, tgt, table):
    rows, dim = ar.shape
    nblk = table.shape[0] // TV
    lanes = -(-rows // 128) * 128
    return pl.pallas_call(
        functools.partial(scores_kernel, nblk),
        out_shape=jax.ShapeDtypeStruct((8, lanes), F32),
        in_specs=[vspec()] * 5 + [aspec()],
        out_specs=vspec(),
        scratch_shapes=[
            pltpu.VMEM((rows, dim), BF16), pltpu.VMEM((EBUF, TV, dim), BF16),
            pltpu.VMEM((rows, TV), F32), pltpu.VMEM((rows, TV), F32),
            pltpu.VMEM((rows, 128), F32), pltpu.VMEM((rows, 128), F32), pltpu.VMEM((rows, 128), F32),
            pltpu.SemaphoreType.DMA((EBUF,)),
        ],
        compiler_params=pltpu.CompilerParams(vmem_limit_bytes=32 * MIB),
        name="table_scores",
    )(ar, prev, ln, nf, tgt, table)


def combine_kernel(x_ref, out_ref, got, ssem, rsem):
    dp = lax.axis_index("dp")
    tp = lax.axis_index("tp")
    barrier = pltpu.get_barrier_semaphore()
    for d in range(1, 4):
        pl.semaphore_signal(barrier, inc=1, device_id=(dp, lax.rem(tp + d, 4)), device_id_type=MESH)
    pl.semaphore_wait(barrier, 3)
    sends = []
    for d in range(1, 4):
        sends.append(pltpu.make_async_remote_copy(src_ref=x_ref, dst_ref=got.at[d - 1], send_sem=ssem.at[d - 1], recv_sem=rsem.at[d - 1],
                                                  device_id=(dp, lax.rem(tp + d, 4)), device_id_type=MESH))
        sends[-1].start()
    for s in sends:
        s.wait()
    mine = x_ref[...]
    vals = [mine] + [got[d] for d in range(3)]
    ordered = []
    for dev in range(4):
        v = mine
        for d in range(1, 4):
            v = jnp.where(lax.rem(tp + 4 - d, 4) == dev, vals[d], v)
        ordered.append(v)
    top = jnp.maximum(jnp.maximum(ordered[0][0:1], ordered[1][0:1]), jnp.maximum(ordered[2][0:1], ordered[3][0:1]))
    tot = 0.0
    tgt = 0.0
    for v in ordered:
        tot = tot + v[1:2] * jnp.exp(v[0:1] - top)
        tgt = tgt + v[2:3]
    log_z = top + jnp.log(tot)
    lanes = out_ref.shape[1]
    row = lax.broadcasted_iota(jnp.int32, (8, lanes), 0)
    out_ref[...] = jnp.where(row == 0, tgt - log_z, log_z)


def combine(x, cid):
    return pl.pallas_call(
        combine_kernel,
        out_shape=jax.ShapeDtypeStruct(x.shape, F32),
        in_specs=[vspec()],
        out_specs=vspec(),
        scratch_shapes=[pltpu.VMEM((3,) + x.shape, F32), pltpu.SemaphoreType.DMA((3,)), pltpu.SemaphoreType.DMA((3,))],
        compiler_params=pltpu.CompilerParams(collective_id=cid, has_side_effects=True),
        name="combine_tp",
    )(x)


def solution(mesh):
    arg_specs = (P('dp', None), P('dp', None), P('dp'), P('tp', None), P(), P(), P(), P(), P(), P(), P(None, None, 'tp'), P(None, None, 'tp'), P(None, 'tp', None), P(), P(None, 'dp'), P(None, 'dp'))
    result_specs = (P('dp', None), P('dp', None), P(None, 'dp'), P(None, 'dp'))

    def decode_local(tokens, targets, start_pos, embed_table, layer_norms, w_q, w_k, w_v, qk_norms, w_o, w_gate, w_up, w_down, norm_final, k_cache, v_cache):
        batch, steps = tokens.shape
        layers, dim, heads, head_dim = w_q.shape
        window = k_cache.shape[2]
        vocab_local = embed_table.shape[0]
        rows = batch * steps
        vocab_start = lax.axis_index('tp') * vocab_local
        def by_row(x):
            return jnp.swapaxes(x.reshape(2, batch // 2, steps), 1, 2).reshape(rows)

        def from_row(x):
            return jnp.swapaxes(x.reshape(2, steps, batch // 2), 1, 2).reshape(batch, steps)

        core = (lax.axis_index('tp') % 2).reshape(1)
        positions = by_row(start_pos[:, None] + jnp.arange(steps)[None, :])
        inv_freq = ROPE_BASE ** (-2.0 * jnp.arange(head_dim // 2, dtype=F32) / head_dim)
        angles = positions.astype(F32)[:, None] * inv_freq[None, :]
        startv = jnp.broadcast_to(start_pos[:, None, None], (batch, 16, 128)).reshape(batch * 16, 128)
        ln = layer_norms.reshape(layers * 4, dim)
        small = (core, start_pos, startv, jnp.cos(angles), jnp.sin(angles), ln, qk_norms.reshape(layers * 2, head_dim))
        qkv = (w_q.reshape(layers, dim, heads * head_dim), w_k.reshape(layers, dim, head_dim), w_v.reshape(layers, dim, head_dim))
        ffn = (w_o.reshape(layers, heads * head_dim, dim), jnp.swapaxes(w_gate, 1, 2), jnp.swapaxes(w_up, 1, 2), w_down)
        caches = (k_cache.reshape(layers, batch, window, head_dim), v_cache.reshape(layers, batch, window, head_dim))
        ar = share(pair_sum(gather_rows(by_row(tokens) - vocab_start, embed_table), 0), 1)
        hid, outs = None, None
        for layer in range(layers):
            hid, own_heads, fresh, *outs = attend(layer, small, ar, hid, qkv, caches, outs)
            hid, half = feed(layer, own_heads, hid, ln, ffn, 2 + layer)
            outs = carry_other(layer, steps, core, start_pos, fresh, caches, outs)
            ar = share(half, 4 + layer)
        tgt = (by_row(targets) - vocab_start)[:, None] - jnp.arange(LANES)[None, :]
        stats = table_scores(ar, hid, ln, norm_final.reshape(1, dim), tgt, embed_table)
        res = combine(stats, 4 + layers)
        return from_row(res[0, :rows]), from_row(res[1, :rows]), outs[0].reshape(k_cache.shape), outs[1].reshape(v_cache.shape)

    return jax.shard_map(decode_local, mesh=mesh, in_specs=arg_specs, out_specs=result_specs, check_vma=False)
```

time: 261 us -> 214 us (0.82)
  Pallas kernels: 235 us -> 187 us
  local copies, waits for them, and re-layouts: 20.6 us -> 13.1 us
  waiting for transfers between devices: 0 us -> 5.3 us
  starting transfers between devices: 0 us -> 5.23 us
    pallas_call x5 -> x10, Pallas kernels: 155 us -> 108 us  [the longest x2 38.5 us: attend(): pl.pallas_call(functools.partial(attend_kernel, layer, rows // batch, nor...]
    unnamed x20 -> x18, local copies, waits for them, and re-layouts: 6.01 us -> 0.64 us
    ppermute x0 -> x3, waiting for transfers between devices: none -> 5.3 us  [share(): far = lax.ppermute(half, 'tp', [(n, (n + 2) % 4) for n in range(4)])]
    ppermute x0 -> x3, starting transfers between devices: none -> 5.23 us  [share(): far = lax.ppermute(half, 'tp', [(n, (n + 2) % 4) for n in range(4)])]
  transfers between devices with their start and end apart: 0 -> 3, of which waited for: 0 -> 1; matrix products, arithmetic and copies ran while one was open for 0% -> 5% of each run, Pallas kernels for 0% -> 17%
where the time goes in v2:
time: 214 us
  Pallas kernels  187 us (87%)
  local copies, waits for them, and re-layouts  13.1 us (6%)
  waiting for transfers between devices  5.3 us (2%)
  starting transfers between devices  5.23 us (2%)
  other arithmetic  2.2 us (1%)
    pallas_call x1, Pallas kernels, table_scores(): pl.pallas_call(functools.partial(scores_kernel, nblk), out_shape=jax.Shap...  63.6 us
    pallas_call x2, Pallas kernels, attend(): pl.pallas_call(functools.partial(attend_kernel, layer, rows // batch, nor...  38.5 us
    pallas_call x2, Pallas kernels, carry_other(): pl.pallas_call(functools.partial(carry_kernel, layer, steps), out_shape=c...  36.6 us
    pallas_call x2, Pallas kernels, feed(): pl.pallas_call(functools.partial(feed_kernel, layer), out_shape=[jax.Shap...  22.5 us
    pallas_call x1, Pallas kernels, gather_rows(): pl.pallas_call(functools.partial(gather_kernel, rows), out_shape=jax.Shap...  10.5 us
    pallas_call x4, Pallas kernels, pair_call(): pl.pallas_call(kernel, out_shape=jax.ShapeDtypeStruct((out_rows, dim), F3...  10.2 us
    reshape x1, local copies, waits for them, and re-layouts, decode_local(): w_q.reshape(layers, dim, heads * head_dim)  8.85 us
    ppermute x3, waiting for transfers between devices, share(): far = lax.ppermute(half, 'tp', [(n, (n + 2) % 4) for n in range(4)])  5.3 us
  transfers between devices with their start and end apart: 3, of which 1 were waited for; matrix products, arithmetic and copies ran while one was open for 5% of the time, Pallas kernels for 17%

profile of v2, /device:TPU:0, one launch (start us, length us, event | category | flops | bytes accessed | tf_op | source)
XLA Modules:
  0.0 213.7 jit_solution(10505422797568522683)
XLA Ops:
  0.6 0.7 compare_and_fusion
  1.3 0.7 subtract_clamp_fusion
  2.0 0.1 min.18
  2.1 0.1 min.22
  2.2 0.1 min.20
  2.3 0.1 reshape.222
  2.4 0.1 and.70
  2.6 0.1 fusion.2.col_ref
  2.7 0.0 copy-start.3
  2.7 0.0 copy-start.4
  2.7 10.5 %token_rows.1.part_ref = f32[288,1152]{1,0:T(8,128)S(1)} custom-call(s32[288]{0:T(512)S(1)} %add_select_fusion.2.grp_ref, s32[288,1]{1,0:T(8,128)S(1)} %fusion.2.col_ref, bf16[65536,1152]{1,0:T(8,128)(2,1)} %e_hbm.1), custom_call_target="tpu_custom_call" | custom-call | tf_op jit(solution)/shard_map/token_rows/pallas_call | solution.py:58
  13.2 2.2 %pair_sum.1.a_ref = f32[144,1152]{1,0:T(8,128)S(1)} custom-call(f32[288,1152]{1,0:T(8,128)S(1)} %token_rows.1.part_ref), custom_call_target="tpu_custom_call" | custom-call | tf_op jit(solution)/shard_map/pair_sum/pallas_call | solution.py:123
  15.4 3.1 %collective-permute-start = (f32[144,1152]{1,0:T(8,128)S(1)}, f32[144,1152]{1,0:T(8,128)}, u32[]{:S(2)}, u32[]{:S(2)}) collective-permute-start(f32[144,1152]{1,0:T(8,128)S(1)} %pair_sum.1.a_ref), channel_id=1, source_target_pairs={{0,2},{1,3},{2,0},{3,1},{4,6},{5,7},{6,4},{7,5},{8,10},{9,11},{10,... | collective-permute-start | bytes 1990664 | tf_op jit(solution)/shard_map/ppermute | solution.py:140
  18.5 0.0 copy-done.3
  18.5 0.1 add.61
  18.6 0.0 copy-done.4
  18.6 0.1 convert_element_type.11
  18.7 0.0 copy-start.6
  18.7 0.0 copy-start.5
  18.7 0.0 copy-start
  18.7 0.0 copy-start.1
  18.8 8.9 %reshape.211.refs_8_.refs_9_ = bf16[2,1152,1024]{2,1,0:T(8,128)(2,1)} reshape(bf16[2,1152,4,256]{3,2,1,0:T(4,128)(2,1)} %param.21) | data formatting | bytes 9437184 | tf_op jit(solution)/shard_map/reshape | solution.py:625
  27.6 0.1 broadcast_in_dim.10
  27.7 0.1 broadcast_in_dim.11
  27.8 0.0 copy-done.6
  27.8 0.1 sub.59
  27.9 0.1 sub.61
  28.0 0.0 copy-done.5
  28.0 0.1 iota_subtract_fusion.tgt_ref
  28.1 0.6 multiply_sine_fusion
  28.7 5.3 %collective-permute-done.b_ref = f32[144,1152]{1,0:T(8,128)} collective-permute-done((f32[144,1152]{1,0:T(8,128)S(1)}, f32[144,1152]{1,0:T(8,128)}, u32[]{:S(2)}, u32[]{:S(2)}) %collective-permute-start) | collective-permute-done | bytes 663584 | tf_op jit(solution)/shard_map/ppermute | solution.py:140
  34.0 0.0 slice-start
  34.0 3.5 %pair_share.3.refs_7_ = f32[288,1152]{1,0:T(8,128)S(1)} custom-call(f32[144,1152]{1,0:T(8,128)S(1)} %pair_sum.1.a_ref, f32[144,1152]{1,0:T(8,128)} %collective-permute-done.b_ref), custom_call_target="tpu_custom_call" | custom-call | tf_op jit(solution)/shard_map/pair_share/pallas_call | solution.py:123
  37.5 0.3 broadcast_in_dim.12.refs_2_
  37.8 0.0 copy-done
  37.8 0.0 copy-done.1
  37.8 0.0 slice-start.1
  37.8 19.3 %attend0.1 = (f32[288,1152]{1,0:T(8,128)S(1)}, f32[144,1024]{1,0:T(8,128)S(1)}, f32[4,768,128]{2,1,0:T(8,128)S(1)}, bf16[2,96,512,256]{3,2,1,0:T(8,128)(2,1)}, bf16[2,96,512,256]{3,2,1,0:T(8,128)(2,1)}) custom-call(s32[1]{0:T(128)} %bitcast.refs_0_.core_ref, s32[96]{0:T(128)S(1)} %copy-done.3, s32[1536,128]{1,0:T(8,128)S(1)} %broadcast_in_dim.12.refs_2_, ...), custom_call_target="tpu_custom_call" | custom-call | tf_op jit(solution)/shard_map/attend0/pallas_call | solution.py:433
  57.1 0.0 slice-done
  57.1 0.0 slice-done.1
  57.1 11.2 %feed0.1 = (f32[288,1152]{1,0:T(8,128)S(1)}, f32[144,1152]{1,0:T(8,128)S(1)}) custom-call(f32[144,1024]{1,0:T(8,128)S(1)} %get-tuple-element.22.heads_ref, f32[288,1152]{1,0:T(8,128)S(1)} %get-tuple-element.23.hid_ref, f32[8,1152]{1,0:T(8,128)S(1)} %reshape.209.refs_5_.ln_ref, bf16[2,1024,1152]{2,1,0:T(8,128)(2,1)S(1)} %bitcast.35, ...), custom_call_target="tpu_custom_call" | custom-call | tf_op jit(solution)/shard_map/feed0/pallas_call | solution.py:300
  68.3 1.8 collective-permute-start.1
  70.1 18.3 %carry0.1 = (bf16[2,96,512,256]{3,2,1,0:T(8,128)(2,1)}, bf16[2,96,512,256]{3,2,1,0:T(8,128)(2,1)}) custom-call(s32[1]{0:T(128)} %bitcast.refs_0_.core_ref, s32[96]{0:T(128)S(1)} %copy-done.3, f32[4,768,128]{2,1,0:T(8,128)S(1)} %get-tuple-element.26.fresh, bf16[2,96,512,256]{3,2,1,0:T(8,128)(2,1)} %bitcast.42, ...), custom_call_target="tpu_custom_call", output_to_operand_aliasing={{0}: (5, {}), {1}: (6, {})} | custom-call | flops 10000000000 | bytes 50331648 | tf_op jit(solution)/shard_map/carry0/pallas_call | solution.py:248
  88.4 0.0 collective-permute-done.1.b_ref
  88.4 2.3 %pair_share.4.refs_7_ = f32[288,1152]{1,0:T(8,128)S(1)} custom-call(f32[144,1152]{1,0:T(8,128)S(1)} %get-tuple-element.24.a_ref, f32[144,1152]{1,0:T(8,128)S(1)} %collective-permute-done.1.b_ref), custom_call_target="tpu_custom_call" | custom-call | tf_op jit(solution)/shard_map/pair_share/pallas_call | solution.py:123
  90.7 19.2 %attend1.1 = (f32[288,1152]{1,0:T(8,128)S(1)}, f32[144,1024]{1,0:T(8,128)S(1)}, f32[4,768,128]{2,1,0:T(8,128)S(1)}, bf16[2,96,512,256]{3,2,1,0:T(8,128)(2,1)}, bf16[2,96,512,256]{3,2,1,0:T(8,128)(2,1)}) custom-call(s32[1]{0:T(128)} %bitcast.refs_0_.core_ref, s32[96]{0:T(128)S(1)} %copy-done.3, ...), custom_call_target="tpu_custom_call", output_to_operand_aliasing={{3}: (14, {}), {4}: (15, {})} | custom-call | tf_op jit(solution)/shard_map/attend1/pallas_call | solution.py:433
  110.0 11.2 %feed1.1 = (f32[288,1152]{1,0:T(8,128)S(1)}, f32[144,1152]{1,0:T(8,128)S(1)}) custom-call(f32[144,1024]{1,0:T(8,128)S(1)} %get-tuple-element.31.heads_ref, f32[288,1152]{1,0:T(8,128)S(1)} %get-tuple-element.32.hid_ref, f32[8,1152]{1,0:T(8,128)S(1)} %reshape.209.refs_5_.ln_ref, bf16[2,1024,1152]{2,1,0:T(8,128)(2,1)S(1)} %bitcast.36, ...), custom_call_target="tpu_custom_call" | custom-call | tf_op jit(solution)/shard_map/feed1/pallas_call | solution.py:300
  121.2 0.3 collective-permute-start.2
  121.5 18.3 %carry1.1 = (bf16[2,96,512,256]{3,2,1,0:T(8,128)(2,1)}, bf16[2,96,512,256]{3,2,1,0:T(8,128)(2,1)}) custom-call(s32[1]{0:T(128)} %bitcast.refs_0_.core_ref, s32[96]{0:T(128)S(1)} %copy-done.3, f32[4,768,128]{2,1,0:T(8,128)S(1)} %get-tuple-element.35.fresh, bf16[2,96,512,256]{3,2,1,0:T(8,128)(2,1)} %bitcast.44, ...), custom_call_target="tpu_custom_call", output_to_operand_aliasing={{0}: (5, {}), {1}: (6, {})} | custom-call | flops 10000000000 | bytes 50331648 | tf_op jit(solution)/shard_map/carry1/pallas_call | solution.py:248
  139.8 0.0 collective-permute-done.2.b_ref
  139.8 2.2 %pair_share.5.ar_ref = f32[288,1152]{1,0:T(8,128)S(1)} custom-call(f32[144,1152]{1,0:T(8,128)S(1)} %get-tuple-element.33.a_ref, f32[144,1152]{1,0:T(8,128)S(1)} %collective-permute-done.2.b_ref), custom_call_target="tpu_custom_call" | custom-call | tf_op jit(solution)/shard_map/pair_share/pallas_call | solution.py:123
  142.1 63.6 %table_scores.1.x_ref = f32[8,384]{1,0:T(8,128)S(1)} custom-call(f32[288,1152]{1,0:T(8,128)S(1)} %pair_share.5.ar_ref, f32[288,1152]{1,0:T(8,128)S(1)} %get-tuple-element.34.prev_ref, f32[8,1152]{1,0:T(8,128)S(1)} %reshape.209.refs_5_.ln_ref, f32[1,1152]{1,0:T(1,128)S(1)} %reshape.217.nf_ref, s32[288,128]{1,0:T(8,128)S(1)} %iota_subtract_fusion.tgt_ref, ...), custom_call_target="tpu_custom_call" | custom-call | tf_op jit(solution)/shard_map/table_scores/pallas_call | solution.py:539
  205.7 0.0 copy-start.2
  205.7 0.6 copy-done.2
  206.3 5.1 %combine_tp.1 = f32[8,384]{1,0:T(8,128)} custom-call(f32[8,384]{1,0:T(8,128)} %copy-done.2), custom_call_target="tpu_custom_call" | custom-call | tf_op jit(solution)/shard_map/combine_tp/pallas_call | solution.py:590
  211.4 0.8 slice_reduce_fusion
  212.2 0.1 reshape_squeeze.6
  212.3 0.7 reshape.218
  213.0 0.1 reshape_squeeze.7
  213.1 0.7 reshape.219
  (12 shorter events, 0.1 us)
Async XLA Ops:
  2.7 15.8 %copy-start.3 = (s32[96]{0:T(128)S(1)}, s32[96]{0:T(128)}, u32[]{:S(2)}) copy-start(s32[96]{0:T(128)} %start_ref.3) | copy-start | bytes 1156
  2.7 15.9 %copy-start.4 = (f32[2,4,1152]{2,1,0:T(4,128)S(1)}, f32[2,4,1152]{2,1,0:T(4,128)}, u32[]{:S(2)}) copy-start(f32[2,4,1152]{2,1,0:T(4,128)} %param.20) | copy-start | bytes 110596
  15.4 18.6 %collective-permute-start = (f32[144,1152]{1,0:T(8,128)S(1)}, f32[144,1152]{1,0:T(8,128)}, u32[]{:S(2)}, u32[]{:S(2)}) collective-permute-start(f32[144,1152]{1,0:T(8,128)S(1)} %pair_sum.1.a_ref), channel_id=1, source_target_pairs={{0,2},{1,3},{2,0},{3,1},{4,6},{5,7},{6,4},{7,5},{8,10},{9,11},{10,... | collective-permute-start | bytes 1990664 | tf_op jit(solution)/shard_map/ppermute | solution.py:140
  18.7 9.0 %copy-start.6 = (f32[2,2,256]{2,1,0:T(2,128)S(1)}, f32[2,2,256]{2,1,0:T(2,128)}, u32[]{:S(2)}) copy-start(f32[2,2,256]{2,1,0:T(2,128)} %param.24) | copy-start | bytes 12292
  18.7 9.2 %copy-start.5 = (f32[1152]{0:T(1024)S(1)}, f32[1152]{0:T(1024)}, u32[]{:S(2)}) copy-start(f32[1152]{0:T(1024)} %param.29) | copy-start | bytes 13828
  18.7 19.0 %copy-start = (bf16[2,1152,1,256]{3,1,2,0:T(8,128)(2,1)S(1)}, bf16[2,1152,1,256]{3,1,2,0:T(8,128)(2,1)}, u32[]{:S(2)}) copy-start(bf16[2,1152,1,256]{3,1,2,0:T(8,128)(2,1)} %param.22) | copy-start | bytes 3538948
  18.7 19.0 %copy-start.1 = (bf16[2,1152,1,256]{3,1,2,0:T(8,128)(2,1)S(1)}, bf16[2,1152,1,256]{3,1,2,0:T(8,128)(2,1)}, u32[]{:S(2)}) copy-start(bf16[2,1152,1,256]{3,1,2,0:T(8,128)(2,1)} %param.23) | copy-start | bytes 3538948
  34.0 23.1 %slice-start = ((s8[4718592]{0:T(1024)(128)(4,1)}), s8[4194304]{0:T(1024)(128)(4,1)S(1)}, s32[]{:S(2)}) async-start(s8[4718592]{0:T(1024)(128)(4,1)} %bitcast.33), calls=%async_computation | async-start | bytes 8388608
  37.8 19.3 %slice-start.1 = ((s8[4718592]{0:T(1024)(128)(4,1)}), s8[524288]{0:T(1024)(128)(4,1)S(1)}, s32[]{:S(2)}) async-start(s8[4718592]{0:T(1024)(128)(4,1)} %bitcast.33), calls=%async_computation.1 | async-start | bytes 1048576
  68.3 20.1 %collective-permute-start.1 = (f32[144,1152]{1,0:T(8,128)S(1)}, f32[144,1152]{1,0:T(8,128)S(1)}, u32[]{:S(2)}, u32[]{:S(2)}) collective-permute-start(f32[144,1152]{1,0:T(8,128)S(1)} %get-tuple-element.24.a_ref), channel_id=1, source_target_pairs={{0,2},{1,3},{2,0},{3,1},{4,6},{5,7},{6,4},{7,5},{8,10},{9,11},{10,... | collective-permute-start | bytes 1990664 | tf_op jit(solution)/shard_map/ppermute | solution.py:140
  121.2 18.6 %collective-permute-start.2 = (f32[144,1152]{1,0:T(8,128)S(1)}, f32[144,1152]{1,0:T(8,128)S(1)}, u32[]{:S(2)}, u32[]{:S(2)}) collective-permute-start(f32[144,1152]{1,0:T(8,128)S(1)} %get-tuple-element.33.a_ref), channel_id=1, source_target_pairs={{0,2},{1,3},{2,0},{3,1},{4,6},{5,7},{6,4},{7,5},{8,10},{9,11},{10,... | collective-permute-start | bytes 1990664 | tf_op jit(solution)/shard_map/ppermute | solution.py:140
  205.7 0.6 copy-start.2

commit v3 on v2

--- a/solution.py
+++ b/solution.py
@@ -53,7 +53,7 @@
     rows = ids.shape[0]
     vocab_local, dim = table.shape
     here = (ids >= 0) & (ids < vocab_local)
-    safe = jnp.clip(ids, 0, vocab_local - 1)
+    safe = ids % vocab_local
     col = jnp.where(here, (jnp.arange(rows) % 32) * 8 + safe % 8, -1)[:, None]
     return pl.pallas_call(
         functools.partial(gather_kernel, rows),
@@ -142,7 +142,7 @@
 
 
 NB = 8
-NBUF = 4
+NBUF = 6
 
 
 class Stream:
@@ -162,41 +162,33 @@
                 for n, (dst, buf) in enumerate(zip(self.targets, self.bufs))]
 
     def begin(self):
-        for i in range(2):
+        for i in range(NBUF):
             for c in self.reads(i, i):
                 c.start()
 
     def run(self, nblk, body):
+        assert nblk == NBUF
+
         def block(i, carry):
-            slot = lax.rem(i, NBUF)
+            slot = i
             for c in self.reads(i, slot):
                 c.wait()
 
             @pl.when(i >= 1)
             def _():
-                for c in self.writes(i - 1, lax.rem(i + NBUF - 1, NBUF)):
-                    c.start()
-
-            @pl.when(i >= 2)
-            def _():
-                for c in self.writes(i - 2, lax.rem(i + NBUF - 2, NBUF)):
-                    c.wait()
-
-            @pl.when(i + 2 < nblk)
-            def _():
-                for c in self.reads(i + 2, lax.rem(i + 2, NBUF)):
+                for c in self.writes(i - 1, i - 1):
                     c.start()
 
             body(i, slot)
             return carry
 
         lax.fori_loop(0, nblk, block, 0)
-        for c in self.writes(nblk - 1, (nblk - 1) % NBUF):
+        for c in self.writes(nblk - 1, nblk - 1):
             c.start()
 
     def end(self, nblk):
-        for i in (nblk - 2, nblk - 1):
-            for c in self.writes(i, i % NBUF):
+        for i in range(nblk):
+            for c in self.writes(i, i):
                 c.wait()
 
     def change(self, i, slot, start_ref, fresh, steps):
@@ -252,7 +244,7 @@
         out_specs=[aspec()] * 2,
         scratch_shapes=stream_scratch(),
         input_output_aliases={5: 0, 6: 1},
-        compiler_params=pltpu.CompilerParams(vmem_limit_bytes=24 * MIB),
+        compiler_params=pltpu.CompilerParams(vmem_limit_bytes=32 * MIB),
         cost_estimate=pl.CostEstimate(flops=10 ** 10, bytes_accessed=48 * MIB, transcendentals=0),
         name=f"carry{layer}",
     )(core, start, fresh, *caches, *outs)
@@ -442,13 +434,13 @@
             pltpu.SemaphoreType.DMA((3,)), pltpu.SemaphoreType.DMA,
         ] + stream_scratch(),
         input_output_aliases=alias,
-        compiler_params=pltpu.CompilerParams(vmem_limit_bytes=42 * MIB),
+        compiler_params=pltpu.CompilerParams(vmem_limit_bytes=50 * MIB),
         name=f"attend{layer}",
     )(*ins)
 
 
-TV = 1024
-EBUF = 8
+TV = 2048
+EBUF = 6
 
 
 def scores_kernel(nblk, ar_ref, prev_ref, ln_ref, nf_ref, tgt_ref, e_hbm, out_ref, f_ref, ebuf, za, zb, m_ref, s_ref, t_ref, sem):
@@ -547,7 +539,7 @@
             pltpu.VMEM((rows, 128), F32), pltpu.VMEM((rows, 128), F32), pltpu.VMEM((rows, 128), F32),
             pltpu.SemaphoreType.DMA((EBUF,)),
         ],
-        compiler_params=pltpu.CompilerParams(vmem_limit_bytes=32 * MIB),
+        compiler_params=pltpu.CompilerParams(vmem_limit_bytes=46 * MIB),
         name="table_scores",
     )(ar, prev, ln, nf, tgt, table)
 

time: 214 us -> 217 us (1.014)
  local copies, waits for them, and re-layouts: 13.1 us -> 17.7 us
    pallas_call x1, Pallas kernels: 10.5 us -> 4.23 us  [gather_rows(): pl.pallas_call(functools.partial(gather_kernel, rows), out_shape=jax.Shap...]
    unnamed x18 -> x32, local copies, waits for them, and re-layouts: 0.64 us -> 5.44 us
    pallas_call x2, Pallas kernels: 38.5 us -> 42.9 us  [attend(): pl.pallas_call(functools.partial(attend_kernel, layer, rows // batch, nor...]
where the time goes in v3:
time: 217 us; the launch traced here: 216 us
  Pallas kernels  186 us (86%)
  local copies, waits for them, and re-layouts  17.7 us (8%)
  starting transfers between devices  5.15 us (2%)
  waiting for transfers between devices  5.09 us (2%)
    pallas_call x1, Pallas kernels, table_scores(): pl.pallas_call(functools.partial(scores_kernel, nblk), out_shape=jax.Shap...  63.3 us
    pallas_call x2, Pallas kernels, attend(): pl.pallas_call(functools.partial(attend_kernel, layer, rows // batch, nor...  42.9 us
    pallas_call x2, Pallas kernels, carry_other(): pl.pallas_call(functools.partial(carry_kernel, layer, steps), out_shape=c...  36.3 us
    pallas_call x2, Pallas kernels, feed(): pl.pallas_call(functools.partial(feed_kernel, layer), out_shape=[jax.Shap...  23.4 us
    pallas_call x4, Pallas kernels, pair_call(): pl.pallas_call(kernel, out_shape=jax.ShapeDtypeStruct((out_rows, dim), F3...  10.6 us
    reshape x1, local copies, waits for them, and re-layouts, decode_local(): w_q.reshape(layers, dim, heads * head_dim)  8.86 us
    unnamed x32, local copies, waits for them, and re-layouts  5.44 us
    ppermute x3, starting transfers between devices, share(): far = lax.ppermute(half, 'tp', [(n, (n + 2) % 4) for n in range(4)])  5.15 us
  transfers between devices with their start and end apart: 3, of which 1 were waited for; matrix products, arithmetic and copies ran while one was open for 5% of the time, Pallas kernels for 17%

profile of v3, /device:TPU:0, one launch (start us, length us, event | category | flops | bytes accessed | tf_op | source)
XLA Modules:
  0.0 216.3 jit_solution(10842061705930548809)
XLA Ops:
  0.6 0.7 broadcast_subtract_fusion
  1.3 0.1 sub.65
  1.4 0.1 sub.77
  1.6 0.1 sub.67
  1.6 0.2 fusion.2.col_ref
  1.8 0.0 copy-start.10
  1.8 0.0 copy-start.11
  1.8 4.2 %token_rows.1.part_ref = f32[288,1152]{1,0:T(8,128)S(1)} custom-call(s32[288]{0:T(512)S(1)} %add_select_fusion.3.grp_ref, s32[288,1]{1,0:T(8,128)S(1)} %fusion.2.col_ref, bf16[65536,1152]{1,0:T(8,128)(2,1)} %e_hbm.1), custom_call_target="tpu_custom_call" | custom-call | tf_op jit(solution)/shard_map/token_rows/pallas_call | solution.py:58
  6.1 2.6 %pair_sum.1.a_ref = f32[144,1152]{1,0:T(8,128)S(1)} custom-call(f32[288,1152]{1,0:T(8,128)S(1)} %token_rows.1.part_ref), custom_call_target="tpu_custom_call" | custom-call | tf_op jit(solution)/shard_map/pair_sum/pallas_call | solution.py:123
  8.7 2.9 %collective-permute-start = (f32[144,1152]{1,0:T(8,128)S(1)}, f32[144,1152]{1,0:T(8,128)}, u32[]{:S(2)}, u32[]{:S(2)}) collective-permute-start(f32[144,1152]{1,0:T(8,128)S(1)} %pair_sum.1.a_ref), channel_id=1, source_target_pairs={{0,2},{1,3},{2,0},{3,1},{4,6},{5,7},{6,4},{7,5},{8,10},{9,11},{10,... | collective-permute-start | bytes 1990664 | tf_op jit(solution)/shard_map/ppermute | solution.py:140
  11.6 0.0 copy-done.10
  11.6 0.1 add.74
  11.7 0.0 copy-done.11
  11.7 0.1 convert_element_type.11
  11.8 0.0 copy-start.2
  11.8 0.0 copy-start.3
  11.8 8.9 %reshape.220.refs_8_.refs_9_ = bf16[2,1152,1024]{2,1,0:T(8,128)(2,1)} reshape(bf16[2,1152,4,256]{3,2,1,0:T(4,128)(2,1)} %param.21) | data formatting | bytes 9437184 | tf_op jit(solution)/shard_map/reshape | solution.py:617
  20.6 0.1 broadcast_in_dim.10
  20.7 0.1 broadcast_in_dim.11
  20.8 0.0 copy-done.13
  20.8 0.1 sub.71
  20.9 0.1 sub.73
  21.0 0.0 copy-done.12
  21.0 0.1 iota_subtract_fusion.tgt_ref
  21.1 0.6 multiply_sine_fusion
  21.7 5.1 %collective-permute-done.b_ref = f32[144,1152]{1,0:T(8,128)} collective-permute-done((f32[144,1152]{1,0:T(8,128)S(1)}, f32[144,1152]{1,0:T(8,128)}, u32[]{:S(2)}, u32[]{:S(2)}) %collective-permute-start) | collective-permute-done | bytes 663584 | tf_op jit(solution)/shard_map/ppermute | solution.py:140
  26.8 3.5 %pair_share.3.refs_7_ = f32[288,1152]{1,0:T(8,128)S(1)} custom-call(f32[144,1152]{1,0:T(8,128)S(1)} %pair_sum.1.a_ref, f32[144,1152]{1,0:T(8,128)} %collective-permute-done.b_ref), custom_call_target="tpu_custom_call" | custom-call | tf_op jit(solution)/shard_map/pair_share/pallas_call | solution.py:123
  30.4 0.0 copy-start.1
  30.4 1.0 copy-done.1
  31.4 0.3 broadcast_in_dim.12.refs_2_
  31.7 0.0 copy-done.2
  31.7 0.0 copy-done.3
  31.7 0.0 slice-start.1
  31.7 21.3 %attend0.1 = (f32[288,1152]{1,0:T(8,128)}, f32[144,1024]{1,0:T(8,128)S(1)}, f32[4,768,128]{2,1,0:T(8,128)}, bf16[2,96,512,256]{3,2,1,0:T(8,128)(2,1)}, bf16[2,96,512,256]{3,2,1,0:T(8,128)(2,1)}) custom-call(s32[1]{0:T(128)} %bitcast.refs_0_.core_ref, s32[96]{0:T(128)S(1)} %copy-done.10, s32[1536,128]{1,0:T(8,128)S(1)} %broadcast_in_dim.12.refs_2_, ...), custom_call_target="tpu_custom_call" | custom-call | tf_op jit(solution)/shard_map/attend0/pallas_call | solution.py:425
  53.0 0.0 slice-done
  53.0 0.0 slice-done.1
  53.0 0.0 copy-start.8
  53.0 1.3 copy-done.8
  54.4 11.7 %feed0.1 = (f32[288,1152]{1,0:T(8,128)S(1)}, f32[144,1152]{1,0:T(8,128)S(1)}) custom-call(f32[144,1024]{1,0:T(8,128)S(1)} %get-tuple-element.22.heads_ref, f32[288,1152]{1,0:T(8,128)S(1)} %copy-done.8, f32[8,1152]{1,0:T(8,128)S(1)} %reshape.218.refs_5_.ln_ref, bf16[2,1024,1152]{2,1,0:T(8,128)(2,1)S(1)} %bitcast.32, bf16[2,1728,1152]{2,1,0:T(8,128)(2,1)} %bitcast.48, ...), custom_call_target="tpu_custom_call" | custom-call | tf_op jit(solution)/shard_map/feed0/pallas_call | solution.py:292
  66.1 0.0 copy-start.6
  66.1 1.8 collective-permute-start.1
  67.9 0.0 copy-done.5
  67.9 18.1 %carry0.1 = (bf16[2,96,512,256]{3,2,1,0:T(8,128)(2,1)}, bf16[2,96,512,256]{3,2,1,0:T(8,128)(2,1)}) custom-call(s32[1]{0:T(128)} %bitcast.refs_0_.core_ref, s32[96]{0:T(128)S(1)} %copy-done.10, f32[4,768,128]{2,1,0:T(8,128)S(1)} %copy-done.5, bf16[2,96,512,256]{3,2,1,0:T(8,128)(2,1)} %bitcast.39, ...), custom_call_target="tpu_custom_call", output_to_operand_aliasing={{0}: (5, {}), {1}: (6, {})} | custom-call | flops 10000000000 | bytes 50331648 | tf_op jit(solution)/shard_map/carry0/pallas_call | solution.py:240
  86.0 0.0 copy-done.6
  86.0 0.0 collective-permute-done.1.b_ref
  86.0 2.3 %pair_share.4.refs_7_ = f32[288,1152]{1,0:T(8,128)S(1)} custom-call(f32[144,1152]{1,0:T(8,128)S(1)} %get-tuple-element.24.a_ref, f32[144,1152]{1,0:T(8,128)S(1)} %collective-permute-done.1.b_ref), custom_call_target="tpu_custom_call" | custom-call | tf_op jit(solution)/shard_map/pair_share/pallas_call | solution.py:123
  88.3 0.0 copy-start
  88.3 1.1 copy-done
  89.4 21.6 %attend1.1 = (f32[288,1152]{1,0:T(8,128)}, f32[144,1024]{1,0:T(8,128)S(1)}, f32[4,768,128]{2,1,0:T(8,128)}, bf16[2,96,512,256]{3,2,1,0:T(8,128)(2,1)}, bf16[2,96,512,256]{3,2,1,0:T(8,128)(2,1)}) custom-call(s32[1]{0:T(128)} %bitcast.refs_0_.core_ref, s32[96]{0:T(128)S(1)} %copy-done.10, ...), custom_call_target="tpu_custom_call", output_to_operand_aliasing={{3}: (14, {}), {4}: (15, {})} | custom-call | tf_op jit(solution)/shard_map/attend1/pallas_call | solution.py:425
  111.0 0.0 copy-start.7
  111.1 1.3 copy-done.7
  112.4 11.7 %feed1.1 = (f32[288,1152]{1,0:T(8,128)S(1)}, f32[144,1152]{1,0:T(8,128)S(1)}) custom-call(f32[144,1024]{1,0:T(8,128)S(1)} %get-tuple-element.31.heads_ref, f32[288,1152]{1,0:T(8,128)S(1)} %copy-done.7, f32[8,1152]{1,0:T(8,128)S(1)} %reshape.218.refs_5_.ln_ref, bf16[2,1024,1152]{2,1,0:T(8,128)(2,1)S(1)} %bitcast.33, bf16[2,1728,1152]{2,1,0:T(8,128)(2,1)} %bitcast.49, ...), custom_call_target="tpu_custom_call" | custom-call | tf_op jit(solution)/shard_map/feed1/pallas_call | solution.py:292
  124.1 0.5 collective-permute-start.2
  124.6 18.1 %carry1.1 = (bf16[2,96,512,256]{3,2,1,0:T(8,128)(2,1)}, bf16[2,96,512,256]{3,2,1,0:T(8,128)(2,1)}) custom-call(s32[1]{0:T(128)} %bitcast.refs_0_.core_ref, s32[96]{0:T(128)S(1)} %copy-done.10, f32[4,768,128]{2,1,0:T(8,128)S(1)} %copy-done.4, bf16[2,96,512,256]{3,2,1,0:T(8,128)(2,1)} %bitcast.41, ...), custom_call_target="tpu_custom_call", output_to_operand_aliasing={{0}: (5, {}), {1}: (6, {})} | custom-call | flops 10000000000 | bytes 50331648 | tf_op jit(solution)/shard_map/carry1/pallas_call | solution.py:240
  142.7 0.0 collective-permute-done.2.b_ref
  142.8 2.2 %pair_share.5.ar_ref = f32[288,1152]{1,0:T(8,128)S(1)} custom-call(f32[144,1152]{1,0:T(8,128)S(1)} %get-tuple-element.33.a_ref, f32[144,1152]{1,0:T(8,128)S(1)} %collective-permute-done.2.b_ref), custom_call_target="tpu_custom_call" | custom-call | tf_op jit(solution)/shard_map/pair_share/pallas_call | solution.py:123
  145.0 63.3 %table_scores.1.x_ref = f32[8,384]{1,0:T(8,128)S(1)} custom-call(f32[288,1152]{1,0:T(8,128)S(1)} %pair_share.5.ar_ref, f32[288,1152]{1,0:T(8,128)S(1)} %get-tuple-element.34.prev_ref, f32[8,1152]{1,0:T(8,128)S(1)} %reshape.218.refs_5_.ln_ref, f32[1,1152]{1,0:T(1,128)S(1)} %reshape.226.nf_ref, s32[288,128]{1,0:T(8,128)S(1)} %iota_subtract_fusion.tgt_ref, ...), custom_call_target="tpu_custom_call" | custom-call | tf_op jit(solution)/shard_map/table_scores/pallas_call | solution.py:531
  208.3 0.6 copy-done.9
  208.9 5.1 %combine_tp.1 = f32[8,384]{1,0:T(8,128)} custom-call(f32[8,384]{1,0:T(8,128)} %copy-done.9), custom_call_target="tpu_custom_call" | custom-call | tf_op jit(solution)/shard_map/combine_tp/pallas_call | solution.py:582
  214.0 0.8 slice_reduce_fusion
  214.8 0.1 reshape_squeeze.6
  214.9 0.7 reshape.227
  215.6 0.1 reshape_squeeze.7
  215.7 0.7 reshape.228
  (18 shorter events, 0.1 us)
Async XLA Ops:
  1.8 9.7 %copy-start.10 = (s32[96]{0:T(128)S(1)}, s32[96]{0:T(128)}, u32[]{:S(2)}) copy-start(s32[96]{0:T(128)} %start_ref.3) | copy-start | bytes 1156
  1.8 9.8 %copy-start.11 = (f32[2,4,1152]{2,1,0:T(4,128)S(1)}, f32[2,4,1152]{2,1,0:T(4,128)}, u32[]{:S(2)}) copy-start(f32[2,4,1152]{2,1,0:T(4,128)} %param.20) | copy-start | bytes 110596
  8.7 18.1 %collective-permute-start = (f32[144,1152]{1,0:T(8,128)S(1)}, f32[144,1152]{1,0:T(8,128)}, u32[]{:S(2)}, u32[]{:S(2)}) collective-permute-start(f32[144,1152]{1,0:T(8,128)S(1)} %pair_sum.1.a_ref), channel_id=1, source_target_pairs={{0,2},{1,3},{2,0},{3,1},{4,6},{5,7},{6,4},{7,5},{8,10},{9,11},{10,... | collective-permute-start | bytes 1990664 | tf_op jit(solution)/shard_map/ppermute | solution.py:140
  11.8 9.0 %copy-start.13 = (f32[2,2,256]{2,1,0:T(2,128)S(1)}, f32[2,2,256]{2,1,0:T(2,128)}, u32[]{:S(2)}) copy-start(f32[2,2,256]{2,1,0:T(2,128)} %param.24) | copy-start | bytes 12292
  11.8 9.2 %copy-start.12 = (f32[1152]{0:T(1024)S(1)}, f32[1152]{0:T(1024)}, u32[]{:S(2)}) copy-start(f32[1152]{0:T(1024)} %param.29) | copy-start | bytes 13828
  11.8 19.9 %copy-start.2 = (bf16[2,1152,1,256]{3,1,2,0:T(8,128)(2,1)S(1)}, bf16[2,1152,1,256]{3,1,2,0:T(8,128)(2,1)}, u32[]{:S(2)}) copy-start(bf16[2,1152,1,256]{3,1,2,0:T(8,128)(2,1)} %param.22) | copy-start | bytes 3538948
  11.8 19.9 %copy-start.3 = (bf16[2,1152,1,256]{3,1,2,0:T(8,128)(2,1)S(1)}, bf16[2,1152,1,256]{3,1,2,0:T(8,128)(2,1)}, u32[]{:S(2)}) copy-start(bf16[2,1152,1,256]{3,1,2,0:T(8,128)(2,1)} %param.23) | copy-start | bytes 3538948
  26.8 26.2 %slice-start = ((s8[4718592]{0:T(1024)(128)(4,1)}), s8[4194304]{0:T(1024)(128)(4,1)S(1)}, s32[]{:S(2)}) async-start(s8[4718592]{0:T(1024)(128)(4,1)} %bitcast.30), calls=%async_computation | async-start | bytes 8388608
  30.4 1.1 copy-start.1
  31.7 21.3 %slice-start.1 = ((s8[4718592]{0:T(1024)(128)(4,1)}), s8[524288]{0:T(1024)(128)(4,1)S(1)}, s32[]{:S(2)}) async-start(s8[4718592]{0:T(1024)(128)(4,1)} %bitcast.30), calls=%async_computation.1 | async-start | bytes 1048576
  53.0 1.3 copy-start.8
  54.3 13.5 %copy-start.5 = (f32[4,768,128]{2,1,0:T(8,128)S(1)}, f32[4,768,128]{2,1,0:T(8,128)}, u32[]{:S(2)}) copy-start(f32[4,768,128]{2,1,0:T(8,128)} %get-tuple-element.26.fresh) | copy-start | bytes 4718596
  66.1 19.9 %copy-start.6 = (f32[288,1152]{1,0:T(8,128)}, f32[288,1152]{1,0:T(8,128)S(1)}, u32[]{:S(2)}) copy-start(f32[288,1152]{1,0:T(8,128)S(1)} %get-tuple-element.25.refs_8_) | copy-start | bytes 3981316
  66.1 19.9 %collective-permute-start.1 = (f32[144,1152]{1,0:T(8,128)S(1)}, f32[144,1152]{1,0:T(8,128)S(1)}, u32[]{:S(2)}, u32[]{:S(2)}) collective-permute-start(f32[144,1152]{1,0:T(8,128)S(1)} %get-tuple-element.24.a_ref), channel_id=1, source_target_pairs={{0,2},{1,3},{2,0},{3,1},{4,6},{5,7},{6,4},{7,5},{8,10},{9,11},{10,... | collective-permute-start | bytes 1990664 | tf_op jit(solution)/shard_map/ppermute | solution.py:140
  88.3 1.1 copy-start
  111.0 1.3 copy-start.7
  112.4 12.2 %copy-start.4 = (f32[4,768,128]{2,1,0:T(8,128)S(1)}, f32[4,768,128]{2,1,0:T(8,128)}, u32[]{:S(2)}) copy-start(f32[4,768,128]{2,1,0:T(8,128)} %get-tuple-element.35.fresh) | copy-start | bytes 4718596
  124.1 18.6 %collective-permute-start.2 = (f32[144,1152]{1,0:T(8,128)S(1)}, f32[144,1152]{1,0:T(8,128)S(1)}, u32[]{:S(2)}, u32[]{:S(2)}) collective-permute-start(f32[144,1152]{1,0:T(8,128)S(1)} %get-tuple-element.33.a_ref), channel_id=1, source_target_pairs={{0,2},{1,3},{2,0},{3,1},{4,6},{5,7},{6,4},{7,5},{8,10},{9,11},{10,... | collective-permute-start | bytes 1990664 | tf_op jit(solution)/shard_map/ppermute | solution.py:140
  208.3 0.6 copy-start.9

commit v4 on v2

--- a/solution.py
+++ b/solution.py
@@ -53,7 +53,7 @@
     rows = ids.shape[0]
     vocab_local, dim = table.shape
     here = (ids >= 0) & (ids < vocab_local)
-    safe = jnp.clip(ids, 0, vocab_local - 1)
+    safe = ids % vocab_local
     col = jnp.where(here, (jnp.arange(rows) % 32) * 8 + safe % 8, -1)[:, None]
     return pl.pallas_call(
         functools.partial(gather_kernel, rows),
@@ -161,8 +161,8 @@
         return [pltpu.make_async_copy(buf.at[slot], dst.at[self.layer, self.rows(i)], self.osem.at[n, slot])
                 for n, (dst, buf) in enumerate(zip(self.targets, self.bufs))]
 
-    def begin(self):
-        for i in range(2):
+    def begin(self, first, last):
+        for i in range(first, last):
             for c in self.reads(i, i):
                 c.start()
 
@@ -182,7 +182,7 @@
                 for c in self.writes(i - 2, lax.rem(i + NBUF - 2, NBUF)):
                     c.wait()
 
-            @pl.when(i + 2 < nblk)
+            @pl.when((i + 2 >= NBUF) & (i + 2 < nblk))
             def _():
                 for c in self.reads(i + 2, lax.rem(i + 2, NBUF)):
                     c.start()
@@ -239,7 +239,7 @@
     half = fresh.shape[1] // TILE
     nblk = half // NB
     stream = Stream(layer, (1 - core_ref[0]) * half, (k_hbm, v_hbm), (ko_hbm, vo_hbm), (kbuf, vbuf), rsem, osem)
-    stream.begin()
+    stream.begin(0, NBUF)
     stream.run(nblk, lambda i, slot: stream.change(i, slot, start_ref, (wide(fresh, 0, tiles(i)), wide(fresh, 2, tiles(i))), steps))
     stream.end(nblk)
 
@@ -328,7 +328,7 @@
     stream = Stream(layer, core * half, (k_hbm, v_hbm), (ko_hbm, vo_hbm), (kbuf, vbuf), rsem, osem)
     for c in wcopies:
         c.start()
-    stream.begin()
+    stream.begin(0, 2)
 
     if layer == 0:
         hid = ar_ref[...] * normalizer
@@ -340,6 +340,7 @@
     act = rms(hid, ln(layer, 0)).astype(BF16)
     for c in wcopies:
         c.wait()
+    stream.begin(2, NBUF)
 
     def roped(x, weight, at):
         x = rms(x, weight)
@@ -449,16 +450,28 @@
 
 TV = 1024
 EBUF = 8
+PIECES = 2
 
 
 def scores_kernel(nblk, ar_ref, prev_ref, ln_ref, nf_ref, tgt_ref, e_hbm, out_ref, f_ref, ebuf, za, zb, m_ref, s_ref, t_ref, sem):
     rows, dim = f_ref.shape
 
+    cut = TV // PIECES
+
     def fetch(i, slot):
-        return pltpu.make_async_copy(e_hbm.at[pl.ds(pl.multiple_of(i * TV, TV), TV), :], ebuf.at[slot], sem.at[slot])
+        return [pltpu.make_async_copy(e_hbm.at[pl.ds(pl.multiple_of(i * TV + n * cut, cut), cut), :],
+                                      ebuf.at[slot, pl.ds(n * cut, cut), :], sem.at[slot, n]) for n in range(PIECES)]
+
+    def fetch_start(i, slot):
+        for n, c in enumerate(fetch(i, slot)):
+            c.start(priority=n % 2)
+
+    def fetch_wait(i, slot):
+        for c in fetch(i, slot):
+            c.wait()
 
     for i in range(EBUF - 2):
-        fetch(i, i).start()
+        fetch_start(i, i)
     hid = prev_ref[...] + rms(ar_ref[...], ln_ref[7:8, :])
     f_ref[...] = rms(hid, nf_ref[...]).astype(BF16)
     m_ref[...] = jnp.full_like(m_ref, -jnp.inf)
@@ -490,14 +503,14 @@
             t_ref[sl, :] = hit
 
     def prep(i, slot):
-        fetch(i, slot).wait()
+        fetch_wait(i, slot)
 
     def more(i):
         @pl.when(i < nblk)
         def _():
-            fetch(i, lax.rem(i, EBUF)).start()
-
-    fetch(0, 0).wait()
+            fetch_start(i, lax.rem(i, EBUF))
+
+    fetch_wait(0, 0)
     more(EBUF - 2)
     dots(0, za)
 
@@ -545,7 +558,7 @@
             pltpu.VMEM((rows, dim), BF16), pltpu.VMEM((EBUF, TV, dim), BF16),
             pltpu.VMEM((rows, TV), F32), pltpu.VMEM((rows, TV), F32),
             pltpu.VMEM((rows, 128), F32), pltpu.VMEM((rows, 128), F32), pltpu.VMEM((rows, 128), F32),
-            pltpu.SemaphoreType.DMA((EBUF,)),
+            pltpu.SemaphoreType.DMA((EBUF, PIECES)),
         ],
         compiler_params=pltpu.CompilerParams(vmem_limit_bytes=32 * MIB),
         name="table_scores",

time: 214 us -> 203 us (0.949)
  Pallas kernels: 187 us -> 177 us
    pallas_call x1, Pallas kernels: 10.5 us -> 4.16 us  [gather_rows(): pl.pallas_call(functools.partial(gather_kernel, rows), out_shape=jax.Shap...]
    pallas_call x2, Pallas kernels: 38.5 us -> 36.1 us  [attend(): pl.pallas_call(functools.partial(attend_kernel, layer, rows // batch, nor...]
  transfers between devices with their start and end apart: 3 -> 3, of which waited for: 1 -> 1; matrix products, arithmetic and copies ran while one was open for 5% -> 5% of each run, Pallas kernels for 17% -> 18%
where the time goes in v4:
time: 203 us
  Pallas kernels  177 us (87%)
  local copies, waits for them, and re-layouts  12.9 us (6%)
  waiting for transfers between devices  5.09 us (3%)
  starting transfers between devices  4.98 us (2%)
    pallas_call x1, Pallas kernels, table_scores(): pl.pallas_call(functools.partial(scores_kernel, nblk), out_shape=jax.Shap...  62.2 us
    pallas_call x2, Pallas kernels, carry_other(): pl.pallas_call(functools.partial(carry_kernel, layer, steps), out_shape=c...  36.4 us
    pallas_call x2, Pallas kernels, attend(): pl.pallas_call(functools.partial(attend_kernel, layer, rows // batch, nor...  36.1 us
    pallas_call x2, Pallas kernels, feed(): pl.pallas_call(functools.partial(feed_kernel, layer), out_shape=[jax.Shap...  22.9 us
    pallas_call x4, Pallas kernels, pair_call(): pl.pallas_call(kernel, out_shape=jax.ShapeDtypeStruct((out_rows, dim), F3...  10.6 us
    reshape x1, local copies, waits for them, and re-layouts, decode_local(): w_q.reshape(layers, dim, heads * head_dim)  8.85 us
    pallas_call x1, Pallas kernels, combine(): pl.pallas_call(combine_kernel, out_shape=jax.ShapeDtypeStruct(x.shape, F3...  5.1 us
    ppermute x3, waiting for transfers between devices, share(): far = lax.ppermute(half, 'tp', [(n, (n + 2) % 4) for n in range(4)])  5.09 us
  transfers between devices with their start and end apart: 3, of which 1 were waited for; matrix products, arithmetic and copies ran while one was open for 5% of the time, Pallas kernels for 18%

profile of v4, /device:TPU:0, one launch (start us, length us, event | category | flops | bytes accessed | tf_op | source)
XLA Modules:
  0.0 202.9 jit_solution(9057445040380207252)
XLA Ops:
  0.6 0.7 broadcast_subtract_fusion
  1.3 0.1 sub.65
  1.4 0.1 sub.77
  1.6 0.1 sub.67
  1.6 0.2 fusion.2.col_ref
  1.8 0.0 copy-start.3
  1.8 0.0 copy-start.4
  1.8 4.2 %token_rows.1.part_ref = f32[288,1152]{1,0:T(8,128)S(1)} custom-call(s32[288]{0:T(512)S(1)} %add_select_fusion.3.grp_ref, s32[288,1]{1,0:T(8,128)S(1)} %fusion.2.col_ref, bf16[65536,1152]{1,0:T(8,128)(2,1)} %e_hbm.1), custom_call_target="tpu_custom_call" | custom-call | tf_op jit(solution)/shard_map/token_rows/pallas_call | solution.py:58
  6.0 2.6 %pair_sum.1.a_ref = f32[144,1152]{1,0:T(8,128)S(1)} custom-call(f32[288,1152]{1,0:T(8,128)S(1)} %token_rows.1.part_ref), custom_call_target="tpu_custom_call" | custom-call | tf_op jit(solution)/shard_map/pair_sum/pallas_call | solution.py:123
  8.6 2.9 %collective-permute-start = (f32[144,1152]{1,0:T(8,128)S(1)}, f32[144,1152]{1,0:T(8,128)}, u32[]{:S(2)}, u32[]{:S(2)}) collective-permute-start(f32[144,1152]{1,0:T(8,128)S(1)} %pair_sum.1.a_ref), channel_id=1, source_target_pairs={{0,2},{1,3},{2,0},{3,1},{4,6},{5,7},{6,4},{7,5},{8,10},{9,11},{10,... | collective-permute-start | bytes 1990664 | tf_op jit(solution)/shard_map/ppermute | solution.py:140
  11.5 0.0 copy-done.3
  11.5 0.1 add.74
  11.6 0.0 copy-done.4
  11.6 0.1 convert_element_type.11
  11.7 0.0 copy-start.6
  11.7 0.0 copy-start.5
  11.7 0.0 copy-start
  11.7 0.0 copy-start.1
  11.7 8.9 %reshape.220.refs_8_.refs_9_ = bf16[2,1152,1024]{2,1,0:T(8,128)(2,1)} reshape(bf16[2,1152,4,256]{3,2,1,0:T(4,128)(2,1)} %param.21) | data formatting | bytes 9437184 | tf_op jit(solution)/shard_map/reshape | solution.py:638
  20.6 0.1 broadcast_in_dim.10
  20.6 0.1 broadcast_in_dim.11
  20.7 0.0 copy-done.6
  20.8 0.1 sub.71
  20.8 0.1 sub.73
  20.9 0.0 copy-done.5
  21.0 0.1 iota_subtract_fusion.tgt_ref
  21.1 0.6 multiply_sine_fusion
  21.7 5.1 %collective-permute-done.b_ref = f32[144,1152]{1,0:T(8,128)} collective-permute-done((f32[144,1152]{1,0:T(8,128)S(1)}, f32[144,1152]{1,0:T(8,128)}, u32[]{:S(2)}, u32[]{:S(2)}) %collective-permute-start) | collective-permute-done | bytes 663584 | tf_op jit(solution)/shard_map/ppermute | solution.py:140
  26.7 0.0 slice-start
  26.8 3.5 %pair_share.3.refs_7_ = f32[288,1152]{1,0:T(8,128)S(1)} custom-call(f32[144,1152]{1,0:T(8,128)S(1)} %pair_sum.1.a_ref, f32[144,1152]{1,0:T(8,128)} %collective-permute-done.b_ref), custom_call_target="tpu_custom_call" | custom-call | tf_op jit(solution)/shard_map/pair_share/pallas_call | solution.py:123
  30.3 0.3 broadcast_in_dim.12.refs_2_
  30.5 0.0 copy-done
  30.6 0.0 copy-done.1
  30.6 0.0 slice-start.1
  30.6 18.1 %attend0.1 = (f32[288,1152]{1,0:T(8,128)S(1)}, f32[144,1024]{1,0:T(8,128)S(1)}, f32[4,768,128]{2,1,0:T(8,128)S(1)}, bf16[2,96,512,256]{3,2,1,0:T(8,128)(2,1)}, bf16[2,96,512,256]{3,2,1,0:T(8,128)(2,1)}) custom-call(s32[1]{0:T(128)} %bitcast.refs_0_.core_ref, s32[96]{0:T(128)S(1)} %copy-done.3, s32[1536,128]{1,0:T(8,128)S(1)} %broadcast_in_dim.12.refs_2_, ...), custom_call_target="tpu_custom_call" | custom-call | tf_op jit(solution)/shard_map/attend0/pallas_call | solution.py:434
  48.6 0.0 slice-done
  48.7 0.0 slice-done.1
  48.7 11.3 %feed0.1 = (f32[288,1152]{1,0:T(8,128)S(1)}, f32[144,1152]{1,0:T(8,128)S(1)}) custom-call(f32[144,1024]{1,0:T(8,128)S(1)} %get-tuple-element.22.heads_ref, f32[288,1152]{1,0:T(8,128)S(1)} %get-tuple-element.23.hid_ref, f32[8,1152]{1,0:T(8,128)S(1)} %reshape.218.refs_5_.ln_ref, bf16[2,1024,1152]{2,1,0:T(8,128)(2,1)S(1)} %bitcast.32, ...), custom_call_target="tpu_custom_call" | custom-call | tf_op jit(solution)/shard_map/feed0/pallas_call | solution.py:300
  59.9 1.8 collective-permute-start.1
  61.7 18.2 %carry0.1 = (bf16[2,96,512,256]{3,2,1,0:T(8,128)(2,1)}, bf16[2,96,512,256]{3,2,1,0:T(8,128)(2,1)}) custom-call(s32[1]{0:T(128)} %bitcast.refs_0_.core_ref, s32[96]{0:T(128)S(1)} %copy-done.3, f32[4,768,128]{2,1,0:T(8,128)S(1)} %get-tuple-element.26.fresh, bf16[2,96,512,256]{3,2,1,0:T(8,128)(2,1)} %bitcast.39, ...), custom_call_target="tpu_custom_call", output_to_operand_aliasing={{0}: (5, {}), {1}: (6, {})} | custom-call | flops 10000000000 | bytes 50331648 | tf_op jit(solution)/shard_map/carry0/pallas_call | solution.py:248
  79.9 0.0 collective-permute-done.1.b_ref
  80.0 2.3 %pair_share.4.refs_7_ = f32[288,1152]{1,0:T(8,128)S(1)} custom-call(f32[144,1152]{1,0:T(8,128)S(1)} %get-tuple-element.24.a_ref, f32[144,1152]{1,0:T(8,128)S(1)} %collective-permute-done.1.b_ref), custom_call_target="tpu_custom_call" | custom-call | tf_op jit(solution)/shard_map/pair_share/pallas_call | solution.py:123
  82.2 18.1 %attend1.1 = (f32[288,1152]{1,0:T(8,128)S(1)}, f32[144,1024]{1,0:T(8,128)S(1)}, f32[4,768,128]{2,1,0:T(8,128)S(1)}, bf16[2,96,512,256]{3,2,1,0:T(8,128)(2,1)}, bf16[2,96,512,256]{3,2,1,0:T(8,128)(2,1)}) custom-call(s32[1]{0:T(128)} %bitcast.refs_0_.core_ref, s32[96]{0:T(128)S(1)} %copy-done.3, ...), custom_call_target="tpu_custom_call", output_to_operand_aliasing={{3}: (14, {}), {4}: (15, {})} | custom-call | tf_op jit(solution)/shard_map/attend1/pallas_call | solution.py:434
  100.3 11.6 %feed1.1 = (f32[288,1152]{1,0:T(8,128)S(1)}, f32[144,1152]{1,0:T(8,128)S(1)}) custom-call(f32[144,1024]{1,0:T(8,128)S(1)} %get-tuple-element.31.heads_ref, f32[288,1152]{1,0:T(8,128)S(1)} %get-tuple-element.32.hid_ref, f32[8,1152]{1,0:T(8,128)S(1)} %reshape.218.refs_5_.ln_ref, bf16[2,1024,1152]{2,1,0:T(8,128)(2,1)S(1)} %bitcast.33, ...), custom_call_target="tpu_custom_call" | custom-call | tf_op jit(solution)/shard_map/feed1/pallas_call | solution.py:300
  111.9 0.3 collective-permute-start.2
  112.2 18.2 %carry1.1 = (bf16[2,96,512,256]{3,2,1,0:T(8,128)(2,1)}, bf16[2,96,512,256]{3,2,1,0:T(8,128)(2,1)}) custom-call(s32[1]{0:T(128)} %bitcast.refs_0_.core_ref, s32[96]{0:T(128)S(1)} %copy-done.3, f32[4,768,128]{2,1,0:T(8,128)S(1)} %get-tuple-element.35.fresh, bf16[2,96,512,256]{3,2,1,0:T(8,128)(2,1)} %bitcast.41, ...), custom_call_target="tpu_custom_call", output_to_operand_aliasing={{0}: (5, {}), {1}: (6, {})} | custom-call | flops 10000000000 | bytes 50331648 | tf_op jit(solution)/shard_map/carry1/pallas_call | solution.py:248
  130.5 0.0 collective-permute-done.2.b_ref
  130.5 2.2 %pair_share.5.ar_ref = f32[288,1152]{1,0:T(8,128)S(1)} custom-call(f32[144,1152]{1,0:T(8,128)S(1)} %get-tuple-element.33.a_ref, f32[144,1152]{1,0:T(8,128)S(1)} %collective-permute-done.2.b_ref), custom_call_target="tpu_custom_call" | custom-call | tf_op jit(solution)/shard_map/pair_share/pallas_call | solution.py:123
  132.7 62.2 %table_scores.1.x_ref = f32[8,384]{1,0:T(8,128)S(1)} custom-call(f32[288,1152]{1,0:T(8,128)S(1)} %pair_share.5.ar_ref, f32[288,1152]{1,0:T(8,128)S(1)} %get-tuple-element.34.prev_ref, f32[8,1152]{1,0:T(8,128)S(1)} %reshape.218.refs_5_.ln_ref, f32[1,1152]{1,0:T(1,128)S(1)} %reshape.226.nf_ref, s32[288,128]{1,0:T(8,128)S(1)} %iota_subtract_fusion.tgt_ref, ...), custom_call_target="tpu_custom_call" | custom-call | tf_op jit(solution)/shard_map/table_scores/pallas_call | solution.py:552
  194.9 0.0 copy-start.2
  194.9 0.6 copy-done.2
  195.5 5.1 %combine_tp.1 = f32[8,384]{1,0:T(8,128)} custom-call(f32[8,384]{1,0:T(8,128)} %copy-done.2), custom_call_target="tpu_custom_call" | custom-call | tf_op jit(solution)/shard_map/combine_tp/pallas_call | solution.py:603
  200.6 0.8 slice_reduce_fusion
  201.4 0.1 reshape_squeeze.6
  201.5 0.7 reshape.227
  202.2 0.1 reshape_squeeze.7
  202.3 0.7 reshape.228
  (11 shorter events, 0.1 us)
Async XLA Ops:
  1.8 9.7 %copy-start.3 = (s32[96]{0:T(128)S(1)}, s32[96]{0:T(128)}, u32[]{:S(2)}) copy-start(s32[96]{0:T(128)} %start_ref.3) | copy-start | bytes 1156
  1.8 9.8 %copy-start.4 = (f32[2,4,1152]{2,1,0:T(4,128)S(1)}, f32[2,4,1152]{2,1,0:T(4,128)}, u32[]{:S(2)}) copy-start(f32[2,4,1152]{2,1,0:T(4,128)} %param.20) | copy-start | bytes 110596
  8.6 18.1 %collective-permute-start = (f32[144,1152]{1,0:T(8,128)S(1)}, f32[144,1152]{1,0:T(8,128)}, u32[]{:S(2)}, u32[]{:S(2)}) collective-permute-start(f32[144,1152]{1,0:T(8,128)S(1)} %pair_sum.1.a_ref), channel_id=1, source_target_pairs={{0,2},{1,3},{2,0},{3,1},{4,6},{5,7},{6,4},{7,5},{8,10},{9,11},{10,... | collective-permute-start | bytes 1990664 | tf_op jit(solution)/shard_map/ppermute | solution.py:140
  11.7 9.0 %copy-start.6 = (f32[2,2,256]{2,1,0:T(2,128)S(1)}, f32[2,2,256]{2,1,0:T(2,128)}, u32[]{:S(2)}) copy-start(f32[2,2,256]{2,1,0:T(2,128)} %param.24) | copy-start | bytes 12292
  11.7 9.2 %copy-start.5 = (f32[1152]{0:T(1024)S(1)}, f32[1152]{0:T(1024)}, u32[]{:S(2)}) copy-start(f32[1152]{0:T(1024)} %param.29) | copy-start | bytes 13828
  11.7 18.9 %copy-start = (bf16[2,1152,1,256]{3,1,2,0:T(8,128)(2,1)S(1)}, bf16[2,1152,1,256]{3,1,2,0:T(8,128)(2,1)}, u32[]{:S(2)}) copy-start(bf16[2,1152,1,256]{3,1,2,0:T(8,128)(2,1)} %param.22) | copy-start | bytes 3538948
  11.7 18.9 %copy-start.1 = (bf16[2,1152,1,256]{3,1,2,0:T(8,128)(2,1)S(1)}, bf16[2,1152,1,256]{3,1,2,0:T(8,128)(2,1)}, u32[]{:S(2)}) copy-start(bf16[2,1152,1,256]{3,1,2,0:T(8,128)(2,1)} %param.23) | copy-start | bytes 3538948
  26.7 21.9 %slice-start = ((s8[4718592]{0:T(1024)(128)(4,1)}), s8[4194304]{0:T(1024)(128)(4,1)S(1)}, s32[]{:S(2)}) async-start(s8[4718592]{0:T(1024)(128)(4,1)} %bitcast.30), calls=%async_computation | async-start | bytes 8388608
  30.6 18.1 %slice-start.1 = ((s8[4718592]{0:T(1024)(128)(4,1)}), s8[524288]{0:T(1024)(128)(4,1)S(1)}, s32[]{:S(2)}) async-start(s8[4718592]{0:T(1024)(128)(4,1)} %bitcast.30), calls=%async_computation.1 | async-start | bytes 1048576
  59.9 20.0 %collective-permute-start.1 = (f32[144,1152]{1,0:T(8,128)S(1)}, f32[144,1152]{1,0:T(8,128)S(1)}, u32[]{:S(2)}, u32[]{:S(2)}) collective-permute-start(f32[144,1152]{1,0:T(8,128)S(1)} %get-tuple-element.24.a_ref), channel_id=1, source_target_pairs={{0,2},{1,3},{2,0},{3,1},{4,6},{5,7},{6,4},{7,5},{8,10},{9,11},{10,... | collective-permute-start | bytes 1990664 | tf_op jit(solution)/shard_map/ppermute | solution.py:140
  111.9 18.5 %collective-permute-start.2 = (f32[144,1152]{1,0:T(8,128)S(1)}, f32[144,1152]{1,0:T(8,128)S(1)}, u32[]{:S(2)}, u32[]{:S(2)}) collective-permute-start(f32[144,1152]{1,0:T(8,128)S(1)} %get-tuple-element.33.a_ref), channel_id=1, source_target_pairs={{0,2},{1,3},{2,0},{3,1},{4,6},{5,7},{6,4},{7,5},{8,10},{9,11},{10,... | collective-permute-start | bytes 1990664 | tf_op jit(solution)/shard_map/ppermute | solution.py:140
  194.9 0.6 copy-start.2

commit v5 on v4

--- a/solution.py
+++ b/solution.py
@@ -276,7 +276,7 @@
     hid = hid_ref[...] + rms(jnp.dot(x, wo[...], preferred_element_type=F32), ln(1))
     hid_out[...] = hid
     act = rms(hid, ln(2)).astype(BF16)
-    for c in wcopies[1:]:
+    for c in wcopies[1:3]:
         c.wait()
     width = wg.shape[0]
     for at in range(0, width, WINDOW):
@@ -284,6 +284,8 @@
         gate = lax.dot_general(act, wg[cut, :], NT, preferred_element_type=F32)
         up = lax.dot_general(act, wu[cut, :], NT, preferred_element_type=F32)
         inner = (jax.nn.gelu(gate, approximate=True) * up).astype(BF16)
+        if at == 0:
+            wcopies[3].wait()
         down = jnp.dot(inner, wd[cut, :], preferred_element_type=F32)
         if at == 0:
             part[...] = down
@@ -479,8 +481,8 @@
     t_ref[...] = jnp.zeros_like(t_ref)
 
     def dots(slot, z):
-        for c in range(TV // 256):
-            z[:, c * 256:(c + 1) * 256] = lax.dot_general(f_ref[...], ebuf[slot, c * 256:(c + 1) * 256, :], NT, preferred_element_type=F32)
+        for c in range(TV // 512):
+            z[:, c * 512:(c + 1) * 512] = lax.dot_general(f_ref[...], ebuf[slot, c * 512:(c + 1) * 512, :], NT, preferred_element_type=F32)
 
     def fold(i, z):
         for r in range(rows // 8):

time: 203 us -> 202 us (level)
  no operation moved by 1% of the time
where the time goes in v5:
time: 202 us; the launch traced here: 201 us
  Pallas kernels  176 us (87%)
  local copies, waits for them, and re-layouts  12.9 us (6%)
  waiting for transfers between devices  5.09 us (3%)
  starting transfers between devices  4.99 us (2%)
    pallas_call x1, Pallas kernels, table_scores(): pl.pallas_call(functools.partial(scores_kernel, nblk), out_shape=jax.Shap...  62.2 us
    pallas_call x2, Pallas kernels, carry_other(): pl.pallas_call(functools.partial(carry_kernel, layer, steps), out_shape=c...  36.4 us
    pallas_call x2, Pallas kernels, attend(): pl.pallas_call(functools.partial(attend_kernel, layer, rows // batch, nor...  36.1 us
    pallas_call x2, Pallas kernels, feed(): pl.pallas_call(functools.partial(feed_kernel, layer), out_shape=[jax.Shap...  21.3 us
    pallas_call x4, Pallas kernels, pair_call(): pl.pallas_call(kernel, out_shape=jax.ShapeDtypeStruct((out_rows, dim), F3...  10.6 us
    reshape x1, local copies, waits for them, and re-layouts, decode_local(): w_q.reshape(layers, dim, heads * head_dim)  8.85 us
    pallas_call x1, Pallas kernels, combine(): pl.pallas_call(combine_kernel, out_shape=jax.ShapeDtypeStruct(x.shape, F3...  5.1 us
    ppermute x3, waiting for transfers between devices, share(): far = lax.ppermute(half, 'tp', [(n, (n + 2) % 4) for n in range(4)])  5.09 us
  transfers between devices with their start and end apart: 3, of which 1 were waited for; matrix products, arithmetic and copies ran while one was open for 5% of the time, Pallas kernels for 18%

profile of v5, /device:TPU:0, one launch (start us, length us, event | category | flops | bytes accessed | tf_op | source)
XLA Modules:
  0.0 201.3 jit_solution(4885107629472694282)
XLA Ops:
  0.6 0.7 broadcast_subtract_fusion
  1.3 0.1 sub.65
  1.4 0.1 sub.77
  1.6 0.1 sub.67
  1.6 0.2 fusion.2.col_ref
  1.8 0.0 copy-start.3
  1.8 0.0 copy-start.4
  1.8 4.0 %token_rows.1.part_ref = f32[288,1152]{1,0:T(8,128)S(1)} custom-call(s32[288]{0:T(512)S(1)} %add_select_fusion.3.grp_ref, s32[288,1]{1,0:T(8,128)S(1)} %fusion.2.col_ref, bf16[65536,1152]{1,0:T(8,128)(2,1)} %e_hbm.1), custom_call_target="tpu_custom_call" | custom-call | tf_op jit(solution)/shard_map/token_rows/pallas_call | solution.py:58
  5.9 2.6 %pair_sum.1.a_ref = f32[144,1152]{1,0:T(8,128)S(1)} custom-call(f32[288,1152]{1,0:T(8,128)S(1)} %token_rows.1.part_ref), custom_call_target="tpu_custom_call" | custom-call | tf_op jit(solution)/shard_map/pair_sum/pallas_call | solution.py:123
  8.5 2.9 %collective-permute-start = (f32[144,1152]{1,0:T(8,128)S(1)}, f32[144,1152]{1,0:T(8,128)}, u32[]{:S(2)}, u32[]{:S(2)}) collective-permute-start(f32[144,1152]{1,0:T(8,128)S(1)} %pair_sum.1.a_ref), channel_id=1, source_target_pairs={{0,2},{1,3},{2,0},{3,1},{4,6},{5,7},{6,4},{7,5},{8,10},{9,11},{10,... | collective-permute-start | bytes 1990664 | tf_op jit(solution)/shard_map/ppermute | solution.py:140
  11.4 0.0 copy-done.3
  11.4 0.1 add.74
  11.5 0.0 copy-done.4
  11.5 0.1 convert_element_type.11
  11.6 0.0 copy-start.6
  11.6 0.0 copy-start.5
  11.6 0.0 copy-start
  11.6 0.0 copy-start.1
  11.6 8.9 %reshape.220.refs_8_.refs_9_ = bf16[2,1152,1024]{2,1,0:T(8,128)(2,1)} reshape(bf16[2,1152,4,256]{3,2,1,0:T(4,128)(2,1)} %param.21) | data formatting | bytes 9437184 | tf_op jit(solution)/shard_map/reshape | solution.py:640
  20.5 0.1 broadcast_in_dim.10
  20.5 0.1 broadcast_in_dim.11
  20.6 0.0 copy-done.6
  20.6 0.1 sub.71
  20.7 0.1 sub.73
  20.8 0.0 copy-done.5
  20.8 0.1 iota_subtract_fusion.tgt_ref
  21.0 0.6 multiply_sine_fusion
  21.5 5.1 %collective-permute-done.b_ref = f32[144,1152]{1,0:T(8,128)} collective-permute-done((f32[144,1152]{1,0:T(8,128)S(1)}, f32[144,1152]{1,0:T(8,128)}, u32[]{:S(2)}, u32[]{:S(2)}) %collective-permute-start) | collective-permute-done | bytes 663584 | tf_op jit(solution)/shard_map/ppermute | solution.py:140
  26.6 0.0 slice-start
  26.6 3.5 %pair_share.3.refs_7_ = f32[288,1152]{1,0:T(8,128)S(1)} custom-call(f32[144,1152]{1,0:T(8,128)S(1)} %pair_sum.1.a_ref, f32[144,1152]{1,0:T(8,128)} %collective-permute-done.b_ref), custom_call_target="tpu_custom_call" | custom-call | tf_op jit(solution)/shard_map/pair_share/pallas_call | solution.py:123
  30.2 0.3 broadcast_in_dim.12.refs_2_
  30.4 0.0 copy-done
  30.4 0.0 copy-done.1
  30.5 0.0 slice-start.1
  30.5 18.1 %attend0.1 = (f32[288,1152]{1,0:T(8,128)S(1)}, f32[144,1024]{1,0:T(8,128)S(1)}, f32[4,768,128]{2,1,0:T(8,128)S(1)}, bf16[2,96,512,256]{3,2,1,0:T(8,128)(2,1)}, bf16[2,96,512,256]{3,2,1,0:T(8,128)(2,1)}) custom-call(s32[1]{0:T(128)} %bitcast.refs_0_.core_ref, s32[96]{0:T(128)S(1)} %copy-done.3, s32[1536,128]{1,0:T(8,128)S(1)} %broadcast_in_dim.12.refs_2_, ...), custom_call_target="tpu_custom_call" | custom-call | tf_op jit(solution)/shard_map/attend0/pallas_call | solution.py:436
  48.5 0.0 slice-done
  48.5 0.0 slice-done.1
  48.6 10.5 %feed0.1 = (f32[288,1152]{1,0:T(8,128)S(1)}, f32[144,1152]{1,0:T(8,128)S(1)}) custom-call(f32[144,1024]{1,0:T(8,128)S(1)} %get-tuple-element.22.heads_ref, f32[288,1152]{1,0:T(8,128)S(1)} %get-tuple-element.23.hid_ref, f32[8,1152]{1,0:T(8,128)S(1)} %reshape.218.refs_5_.ln_ref, bf16[2,1024,1152]{2,1,0:T(8,128)(2,1)S(1)} %bitcast.32, ...), custom_call_target="tpu_custom_call" | custom-call | tf_op jit(solution)/shard_map/feed0/pallas_call | solution.py:302
  59.1 1.8 collective-permute-start.1
  60.8 18.2 %carry0.1 = (bf16[2,96,512,256]{3,2,1,0:T(8,128)(2,1)}, bf16[2,96,512,256]{3,2,1,0:T(8,128)(2,1)}) custom-call(s32[1]{0:T(128)} %bitcast.refs_0_.core_ref, s32[96]{0:T(128)S(1)} %copy-done.3, f32[4,768,128]{2,1,0:T(8,128)S(1)} %get-tuple-element.26.fresh, bf16[2,96,512,256]{3,2,1,0:T(8,128)(2,1)} %bitcast.39, ...), custom_call_target="tpu_custom_call", output_to_operand_aliasing={{0}: (5, {}), {1}: (6, {})} | custom-call | flops 10000000000 | bytes 50331648 | tf_op jit(solution)/shard_map/carry0/pallas_call | solution.py:248
  79.1 0.0 collective-permute-done.1.b_ref
  79.1 2.3 %pair_share.4.refs_7_ = f32[288,1152]{1,0:T(8,128)S(1)} custom-call(f32[144,1152]{1,0:T(8,128)S(1)} %get-tuple-element.24.a_ref, f32[144,1152]{1,0:T(8,128)S(1)} %collective-permute-done.1.b_ref), custom_call_target="tpu_custom_call" | custom-call | tf_op jit(solution)/shard_map/pair_share/pallas_call | solution.py:123
  81.3 18.1 %attend1.1 = (f32[288,1152]{1,0:T(8,128)S(1)}, f32[144,1024]{1,0:T(8,128)S(1)}, f32[4,768,128]{2,1,0:T(8,128)S(1)}, bf16[2,96,512,256]{3,2,1,0:T(8,128)(2,1)}, bf16[2,96,512,256]{3,2,1,0:T(8,128)(2,1)}) custom-call(s32[1]{0:T(128)} %bitcast.refs_0_.core_ref, s32[96]{0:T(128)S(1)} %copy-done.3, ...), custom_call_target="tpu_custom_call", output_to_operand_aliasing={{3}: (14, {}), {4}: (15, {})} | custom-call | tf_op jit(solution)/shard_map/attend1/pallas_call | solution.py:436
  99.4 10.8 %feed1.1 = (f32[288,1152]{1,0:T(8,128)S(1)}, f32[144,1152]{1,0:T(8,128)S(1)}) custom-call(f32[144,1024]{1,0:T(8,128)S(1)} %get-tuple-element.31.heads_ref, f32[288,1152]{1,0:T(8,128)S(1)} %get-tuple-element.32.hid_ref, f32[8,1152]{1,0:T(8,128)S(1)} %reshape.218.refs_5_.ln_ref, bf16[2,1024,1152]{2,1,0:T(8,128)(2,1)S(1)} %bitcast.33, ...), custom_call_target="tpu_custom_call" | custom-call | tf_op jit(solution)/shard_map/feed1/pallas_call | solution.py:302
  110.3 0.3 collective-permute-start.2
  110.6 18.2 %carry1.1 = (bf16[2,96,512,256]{3,2,1,0:T(8,128)(2,1)}, bf16[2,96,512,256]{3,2,1,0:T(8,128)(2,1)}) custom-call(s32[1]{0:T(128)} %bitcast.refs_0_.core_ref, s32[96]{0:T(128)S(1)} %copy-done.3, f32[4,768,128]{2,1,0:T(8,128)S(1)} %get-tuple-element.35.fresh, bf16[2,96,512,256]{3,2,1,0:T(8,128)(2,1)} %bitcast.41, ...), custom_call_target="tpu_custom_call", output_to_operand_aliasing={{0}: (5, {}), {1}: (6, {})} | custom-call | flops 10000000000 | bytes 50331648 | tf_op jit(solution)/shard_map/carry1/pallas_call | solution.py:248
  128.8 0.0 collective-permute-done.2.b_ref
  128.8 2.2 %pair_share.5.ar_ref = f32[288,1152]{1,0:T(8,128)S(1)} custom-call(f32[144,1152]{1,0:T(8,128)S(1)} %get-tuple-element.33.a_ref, f32[144,1152]{1,0:T(8,128)S(1)} %collective-permute-done.2.b_ref), custom_call_target="tpu_custom_call" | custom-call | tf_op jit(solution)/shard_map/pair_share/pallas_call | solution.py:123
  131.1 62.2 %table_scores.1.x_ref = f32[8,384]{1,0:T(8,128)S(1)} custom-call(f32[288,1152]{1,0:T(8,128)S(1)} %pair_share.5.ar_ref, f32[288,1152]{1,0:T(8,128)S(1)} %get-tuple-element.34.prev_ref, f32[8,1152]{1,0:T(8,128)S(1)} %reshape.218.refs_5_.ln_ref, f32[1,1152]{1,0:T(1,128)S(1)} %reshape.226.nf_ref, s32[288,128]{1,0:T(8,128)S(1)} %iota_subtract_fusion.tgt_ref, ...), custom_call_target="tpu_custom_call" | custom-call | tf_op jit(solution)/shard_map/table_scores/pallas_call | solution.py:554
  193.3 0.0 copy-start.2
  193.3 0.6 copy-done.2
  193.9 5.1 %combine_tp.1 = f32[8,384]{1,0:T(8,128)} custom-call(f32[8,384]{1,0:T(8,128)} %copy-done.2), custom_call_target="tpu_custom_call" | custom-call | tf_op jit(solution)/shard_map/combine_tp/pallas_call | solution.py:605
  199.0 0.8 slice_reduce_fusion
  199.8 0.1 reshape_squeeze.6
  199.9 0.7 reshape.227
  200.5 0.1 reshape_squeeze.7
  200.6 0.7 reshape.228
  (11 shorter events, 0.1 us)
Async XLA Ops:
  1.8 9.6 %copy-start.3 = (s32[96]{0:T(128)S(1)}, s32[96]{0:T(128)}, u32[]{:S(2)}) copy-start(s32[96]{0:T(128)} %start_ref.3) | copy-start | bytes 1156
  1.8 9.6 %copy-start.4 = (f32[2,4,1152]{2,1,0:T(4,128)S(1)}, f32[2,4,1152]{2,1,0:T(4,128)}, u32[]{:S(2)}) copy-start(f32[2,4,1152]{2,1,0:T(4,128)} %param.20) | copy-start | bytes 110596
  8.5 18.1 %collective-permute-start = (f32[144,1152]{1,0:T(8,128)S(1)}, f32[144,1152]{1,0:T(8,128)}, u32[]{:S(2)}, u32[]{:S(2)}) collective-permute-start(f32[144,1152]{1,0:T(8,128)S(1)} %pair_sum.1.a_ref), channel_id=1, source_target_pairs={{0,2},{1,3},{2,0},{3,1},{4,6},{5,7},{6,4},{7,5},{8,10},{9,11},{10,... | collective-permute-start | bytes 1990664 | tf_op jit(solution)/shard_map/ppermute | solution.py:140
  11.6 9.0 %copy-start.6 = (f32[2,2,256]{2,1,0:T(2,128)S(1)}, f32[2,2,256]{2,1,0:T(2,128)}, u32[]{:S(2)}) copy-start(f32[2,2,256]{2,1,0:T(2,128)} %param.24) | copy-start | bytes 12292
  11.6 9.2 %copy-start.5 = (f32[1152]{0:T(1024)S(1)}, f32[1152]{0:T(1024)}, u32[]{:S(2)}) copy-start(f32[1152]{0:T(1024)} %param.29) | copy-start | bytes 13828
  11.6 18.9 %copy-start = (bf16[2,1152,1,256]{3,1,2,0:T(8,128)(2,1)S(1)}, bf16[2,1152,1,256]{3,1,2,0:T(8,128)(2,1)}, u32[]{:S(2)}) copy-start(bf16[2,1152,1,256]{3,1,2,0:T(8,128)(2,1)} %param.22) | copy-start | bytes 3538948
  11.6 18.9 %copy-start.1 = (bf16[2,1152,1,256]{3,1,2,0:T(8,128)(2,1)S(1)}, bf16[2,1152,1,256]{3,1,2,0:T(8,128)(2,1)}, u32[]{:S(2)}) copy-start(bf16[2,1152,1,256]{3,1,2,0:T(8,128)(2,1)} %param.23) | copy-start | bytes 3538948
  26.6 21.9 %slice-start = ((s8[4718592]{0:T(1024)(128)(4,1)}), s8[4194304]{0:T(1024)(128)(4,1)S(1)}, s32[]{:S(2)}) async-start(s8[4718592]{0:T(1024)(128)(4,1)} %bitcast.30), calls=%async_computation | async-start | bytes 8388608
  30.5 18.1 %slice-start.1 = ((s8[4718592]{0:T(1024)(128)(4,1)}), s8[524288]{0:T(1024)(128)(4,1)S(1)}, s32[]{:S(2)}) async-start(s8[4718592]{0:T(1024)(128)(4,1)} %bitcast.30), calls=%async_computation.1 | async-start | bytes 1048576
  59.1 20.0 %collective-permute-start.1 = (f32[144,1152]{1,0:T(8,128)S(1)}, f32[144,1152]{1,0:T(8,128)S(1)}, u32[]{:S(2)}, u32[]{:S(2)}) collective-permute-start(f32[144,1152]{1,0:T(8,128)S(1)} %get-tuple-element.24.a_ref), channel_id=1, source_target_pairs={{0,2},{1,3},{2,0},{3,1},{4,6},{5,7},{6,4},{7,5},{8,10},{9,11},{10,... | collective-permute-start | bytes 1990664 | tf_op jit(solution)/shard_map/ppermute | solution.py:140
  110.3 18.6 %collective-permute-start.2 = (f32[144,1152]{1,0:T(8,128)S(1)}, f32[144,1152]{1,0:T(8,128)S(1)}, u32[]{:S(2)}, u32[]{:S(2)}) collective-permute-start(f32[144,1152]{1,0:T(8,128)S(1)} %get-tuple-element.33.a_ref), channel_id=1, source_target_pairs={{0,2},{1,3},{2,0},{3,1},{4,6},{5,7},{6,4},{7,5},{8,10},{9,11},{10,... | collective-permute-start | bytes 1990664 | tf_op jit(solution)/shard_map/ppermute | solution.py:140
  193.3 0.6 copy-start.2
